TPU v7x, 128 devices: a whole 4x4x4 slice. The times are simulated.
128 devices in a mesh: zm: 16 (over y, x), zv: 8 (over z, core).
Axes of the slice: x: 4, y: 4, z: 4, core: 2. Of those that a mesh axis runs over, the one named last changes fastest.
Arguments:
- table: float32 [256, 512, 256], P('zm', 'zv'), may hold values from -6 to 6
- refined: float32 [4, 2048, 16, 1024], P(None, ('zm', 'zv')), may hold values from -18 to 18
- assign: int32 [4, 128, 16], replicated, may hold values from -1 to 2047, as said below
Outputs:
- table_out: float32 [256, 512, 256], P('zm', 'zv')
- block_error: float32 [4, 2048], P(None, ('zm', 'zv'))
- worst: float32 [4], replicated
Inputs may be any that keep to these rules, and one draw needn't show every extreme that they name: `assign`: devices are numbered d = zm index * 8 + zv index; block b is homed on device b // 16, and its home device has the same zv index as the owner d of the slot. In an iteration no block appears twice, at most 1 block of one home device sit in the slots of one owner (reached in every iteration), and some owner of every zv index has all 16 slots filled.
All inputs are finite; a program needn't handle non-finite values.
Results may differ from a plain program's by a relative error of at most 0.0001.
Values sent between devices are 32-bit elements; how exact they have to be, the bound alone decides.
A program may use at most 128 MiB of HBM per device.

v0:
```python
import functools

import jax
import jax.numpy as jnp
from jax import lax
from jax.sharding import Mesh
from jax.sharding import PartitionSpec as P

S = 8
BLOCK_Z = 16
BLOCK_V = 16
BLOCK_C = 8
ITERS = 4
CAP = 1
ZM_ZV = ("zm_0", "zm_1", "zv_0", "zv_1")
ZM = ("zm_0", "zm_1")
ZV = ("zv_0", "zv_1")


precise = lax.Precision.HIGHEST


def one_axis_at_a_time(x, axes):
    return functools.reduce(lax.psum, axes, x)


def over_axes(x, axes):
    return functools.reduce(lax.pmax, axes, x)


def shifted(value, axis, steps):
    count = lax.axis_size(axis)
    first, last = (max(0, -steps), min(count, count - steps))
    return lax.ppermute(value, axis, [(source, source + steps) for source in range(first, last)])


def corner_mean(corner_grid):
    summed = (
        corner_grid[:-1, :-1, :-1]
        + corner_grid[1:, :-1, :-1]
        + corner_grid[:-1, 1:, :-1]
        + corner_grid[1:, 1:, :-1]
    )
    summed = (
        summed
        + corner_grid[:-1, :-1, 1:]
        + corner_grid[1:, :-1, 1:]
        + corner_grid[:-1, 1:, 1:]
        + corner_grid[1:, 1:, 1:]
    )
    return summed * 0.125


def global_stats(total_sq, biggest):
    whole_sum = one_axis_at_a_time(total_sq, ZM_ZV)
    return (whole_sum, over_axes(biggest, ZM_ZV))


def shards(table, refined, assign):
    zm_count = lax.axis_size(ZM)
    zv_count = lax.axis_size(ZV)
    zm_here = lax.axis_index(ZM)
    zv_here = lax.axis_index(ZV)
    table_depth, table_span, table_wide = table.shape
    channels = table_wide // S
    vary_blocks = table_span // BLOCK_V
    prog_blocks = channels // BLOCK_C
    block_count = vary_blocks * prog_blocks
    block_cells = BLOCK_Z * BLOCK_V * BLOCK_C * S
    slot_total = assign.shape[2]
    device_here = zm_here * zv_count + zv_here
    lane_index = jnp.arange(CAP)
    spot_index = jnp.arange(block_count)
    home_index = jnp.arange(zm_count)
    slot_index = jnp.arange(slot_total)
    worst_list = []
    error_list = []
    for iteration in range(ITERS):
        above_row = shifted(table[:1], ZM, -1)
        above_row = jnp.where(zm_here == zm_count - 1, table[-1:], above_row)
        grown = jnp.concatenate([table, above_row], 0)
        beside = shifted(grown[:, :1], ZV, -1)
        beside = jnp.where(zv_here == zv_count - 1, grown[:, -1:], beside)
        grown = jnp.concatenate([grown, beside], 1)
        corner_grid = grown.reshape(table_depth + 1, table_span + 1, channels, S)
        corner_grid = jnp.concatenate([corner_grid, corner_grid[:, :, -1:]], 2)
        centre = corner_mean(corner_grid)
        view = centre.reshape(BLOCK_Z, vary_blocks, BLOCK_V, prog_blocks, BLOCK_C * S)
        slot_plan = assign[iteration].reshape(zm_count, zv_count, slot_total)
        column = lax.dynamic_index_in_dim(slot_plan, zv_here, 1, False)
        mine_mask = (column >= 0) & (column // block_count == device_here)
        placed = jnp.cumsum(mine_mask.astype(jnp.int32), axis=1) - 1
        local_id = column - device_here * block_count
        pick_place = (mine_mask[:, :, None] & (placed[:, :, None] == lane_index)).astype(
            jnp.float32
        )
        pick_local = (local_id[:, :, None] == spot_index).astype(jnp.float32)
        selector = jnp.einsum("oks,okl->osl", pick_place, pick_local, precision=precise)
        filled = jnp.sum(selector, axis=2) > 0.5
        slot_block = (
            jnp.sum(selector * spot_index.astype(jnp.float32), axis=2).astype(jnp.int32).reshape(-1)
        )
        vary_of = slot_block // prog_blocks
        prog_of = slot_block % prog_blocks
        picked = view[:, vary_of, :, prog_of, :]
        local_blocks = picked.reshape(zm_count, CAP, block_cells)
        wanted = lax.dynamic_index_in_dim(column, zm_here, 0, False)
        live_mask = wanted >= 0
        source = wanted // block_count // zv_count
        earlier = (
            (source[:, None] == source[None, :])
            & live_mask[None, :]
            & (slot_index[None, :] < slot_index[:, None])
        )
        rank_slot = jnp.sum(earlier.astype(jnp.int32), axis=1)
        routing = (
            live_mask[:, None, None]
            & (source[:, None, None] == home_index[None, :, None])
            & (rank_slot[:, None, None] == lane_index)
        ).astype(jnp.float32)
        target = refined[iteration].reshape(slot_total, block_cells)
        cell_count = jnp.sum((slot_plan >= 0).astype(jnp.float32)) * block_cells
        packed = jnp.einsum("khp,kx->hpx", routing, target, precision=precise)
        arrived = lax.all_to_all(packed, ZM, split_axis=0, concat_axis=0, tiled=True)
        residual = jnp.where(filled[:, :, None], arrived - local_blocks, jnp.float32(0.0))
        peak_error = jnp.max(jnp.abs(residual), axis=2)
        total_sq, biggest = global_stats(jnp.sum(residual * residual), jnp.max(peak_error))
        weight = 1.0 / (1.0 + jnp.sqrt(total_sq / cell_count))
        slot_change = weight * residual
        errors = jnp.einsum("opl,op->l", selector, peak_error, precision=precise)
        rows_back = slot_change.reshape(zm_count * CAP, BLOCK_Z, BLOCK_V, BLOCK_C * S)
        change_view = jnp.zeros_like(view).at[:, vary_of, :, prog_of, :].add(rows_back)
        table = table + change_view.reshape(table_depth, table_span, table_wide)
        worst_list.append(biggest)
        error_list.append(errors)
    return (table, jnp.stack(error_list), jnp.stack(worst_list))


def solution(mesh):
    split = Mesh(mesh.devices.reshape(4, 4, 4, 2), ("zm_0", "zm_1", "zv_0", "zv_1"))
    in_specs = (P(ZM, ZV, None), P(None, ZM_ZV, None, None), P())
    out_specs = (P(ZM, ZV, None), P(None, ZM_ZV), P())
    return jax.shard_map(
        shards, mesh=split, in_specs=in_specs, out_specs=out_specs, check_vma=False
    )
```

profile of v0, /device:TPU:1, one launch (start us, length us, event | category | flops | bytes accessed | tf_op | source)
XLA Modules:
  0.0 473.1 jit_solution(6104628909205082638)
XLA Ops:
  12.9 9.0 %all-to-all-start = ((f32[16,1,16384]{2,1,0:T(1,128)}), f32[16,1,16384]{2,1,0:T(1,128)S(1)}, u32[]{:S(2)}, u32[]{:S(2)}) async-start(f32[16,1,16384]{2,1,0:T(1,128)} %copy.126), calls=%async_computation | async-start | bytes 2097152 | tf_op jit(solution)/shard_map/all_to_all | solution.py:124
  45.5 7.2 %reshape.1319 = f32[16,4,16,4,64]{2,1,4,3,0:T(4,128)} reshape(f32[16,64,32,8]{1,3,2,0:T(8,128)} %fusion.27) | data formatting | bytes 2097152 | tf_op jit(solution)/shard_map/reshape | solution.py:88
  68.8 9.7 %psum.112 = f32[]{:T(128)} all-reduce(f32[]{:T(128)} %get-tuple-element.63), channel_id=1, replica_groups=mesh['zm_0'=4,'zm_1'=4,'zv_0'=4,'zv_1'=2] {'zm_0'}, use_global_device_ids=true, to_apply=%region_5.6 | all-reduce | flops 1 | bytes 8 | tf_op jit(solution)/shard_map/psum | solution.py:24
  82.9 15.9 %psum.113 = f32[]{:T(128)} all-reduce(f32[]{:T(128)} %psum.112), channel_id=1, replica_groups=mesh['zm_0'=4,'zm_1'=4,'zv_0'=4,'zv_1'=2] {'zm_1'}, use_global_device_ids=true, to_apply=%region_6.7 | all-reduce | flops 1 | bytes 8 | tf_op jit(solution)/shard_map/psum | solution.py:24
  99.4 10.1 %psum.114 = f32[]{:T(128)} all-reduce(f32[]{:T(128)} %psum.113), channel_id=1, replica_groups=mesh['zm_0'=4,'zm_1'=4,'zv_0'=4,'zv_1'=2] {'zv_0'}, use_global_device_ids=true, to_apply=%region_7.8 | all-reduce | flops 1 | bytes 8 | tf_op jit(solution)/shard_map/psum | solution.py:24
  110.0 8.4 %psum.115 = f32[]{:T(128)} all-reduce(f32[]{:T(128)} %psum.114), channel_id=1, replica_groups=mesh['zm_0'=4,'zm_1'=4,'zv_0'=4,'zv_1'=2] {'zv_1'}, use_global_device_ids=true, to_apply=%region_8.9 | all-reduce | flops 1 | bytes 8 | tf_op jit(solution)/shard_map/psum | solution.py:24
  155.1 7.2 %reshape.1324 = f32[16,4,16,4,64]{2,1,4,3,0:T(4,128)} reshape(f32[16,64,32,8]{1,3,2,0:T(8,128)} %fusion.19) | data formatting | bytes 2097152 | tf_op jit(solution)/shard_map/reshape | solution.py:88
  185.3 10.4 %psum.116 = f32[]{:T(128)} all-reduce(f32[]{:T(128)} %get-tuple-element.59), channel_id=1, replica_groups=mesh['zm_0'=4,'zm_1'=4,'zv_0'=4,'zv_1'=2] {'zm_0'}, use_global_device_ids=true, to_apply=%region_16.17 | all-reduce | flops 1 | bytes 8 | tf_op jit(solution)/shard_map/psum | solution.py:24
  195.7 10.3 %psum.117 = f32[]{:T(128)} all-reduce(f32[]{:T(128)} %psum.116), channel_id=1, replica_groups=mesh['zm_0'=4,'zm_1'=4,'zv_0'=4,'zv_1'=2] {'zm_1'}, use_global_device_ids=true, to_apply=%region_17.18 | all-reduce | flops 1 | bytes 8 | tf_op jit(solution)/shard_map/psum | solution.py:24
  206.6 8.3 %psum.118 = f32[]{:T(128)} all-reduce(f32[]{:T(128)} %psum.117), channel_id=1, replica_groups=mesh['zm_0'=4,'zm_1'=4,'zv_0'=4,'zv_1'=2] {'zv_0'}, use_global_device_ids=true, to_apply=%region_18.19 | all-reduce | flops 1 | bytes 8 | tf_op jit(solution)/shard_map/psum | solution.py:24
  215.5 8.3 %psum.119 = f32[]{:T(128)} all-reduce(f32[]{:T(128)} %psum.118), channel_id=1, replica_groups=mesh['zm_0'=4,'zm_1'=4,'zv_0'=4,'zv_1'=2] {'zv_1'}, use_global_device_ids=true, to_apply=%region_19.20 | all-reduce | flops 1 | bytes 8 | tf_op jit(solution)/shard_map/psum | solution.py:24
  260.2 7.2 %reshape.1329 = f32[16,4,16,4,64]{2,1,4,3,0:T(4,128)} reshape(f32[16,64,32,8]{1,3,2,0:T(8,128)} %fusion.11) | data formatting | bytes 2097152 | tf_op jit(solution)/shard_map/reshape | solution.py:88
  283.5 7.1 %psum.120 = f32[]{:T(128)} all-reduce(f32[]{:T(128)} %get-tuple-element.55), channel_id=1, replica_groups=mesh['zm_0'=4,'zm_1'=4,'zv_0'=4,'zv_1'=2] {'zm_0'}, use_global_device_ids=true, to_apply=%region_27.28 | all-reduce | flops 1 | bytes 8 | tf_op jit(solution)/shard_map/psum | solution.py:24
  295.0 15.8 %psum.121 = f32[]{:T(128)} all-reduce(f32[]{:T(128)} %psum.120), channel_id=1, replica_groups=mesh['zm_0'=4,'zm_1'=4,'zv_0'=4,'zv_1'=2] {'zm_1'}, use_global_device_ids=true, to_apply=%region_28.29 | all-reduce | flops 1 | bytes 8 | tf_op jit(solution)/shard_map/psum | solution.py:24
  311.5 7.3 %psum.122 = f32[]{:T(128)} all-reduce(f32[]{:T(128)} %psum.121), channel_id=1, replica_groups=mesh['zm_0'=4,'zm_1'=4,'zv_0'=4,'zv_1'=2] {'zv_0'}, use_global_device_ids=true, to_apply=%region_29.30 | all-reduce | flops 1 | bytes 8 | tf_op jit(solution)/shard_map/psum | solution.py:24
  319.5 8.3 %psum.123 = f32[]{:T(128)} all-reduce(f32[]{:T(128)} %psum.122), channel_id=1, replica_groups=mesh['zm_0'=4,'zm_1'=4,'zv_0'=4,'zv_1'=2] {'zv_1'}, use_global_device_ids=true, to_apply=%region_30.31 | all-reduce | flops 1 | bytes 8 | tf_op jit(solution)/shard_map/psum | solution.py:24
  362.9 7.2 %reshape.1334 = f32[16,4,16,4,64]{2,1,4,3,0:T(4,128)} reshape(f32[16,64,32,8]{1,3,2,0:T(8,128)} %fusion.3) | data formatting | bytes 2097152 | tf_op jit(solution)/shard_map/reshape | solution.py:88
  386.3 9.5 %psum.124 = f32[]{:T(128)} all-reduce(f32[]{:T(128)} %get-tuple-element.51), channel_id=1, replica_groups=mesh['zm_0'=4,'zm_1'=4,'zv_0'=4,'zv_1'=2] {'zm_0'}, use_global_device_ids=true, to_apply=%region_38.39 | all-reduce | flops 1 | bytes 8 | tf_op jit(solution)/shard_map/psum | solution.py:24
  395.9 8.3 %psum.125 = f32[]{:T(128)} all-reduce(f32[]{:T(128)} %psum.124), channel_id=1, replica_groups=mesh['zm_0'=4,'zm_1'=4,'zv_0'=4,'zv_1'=2] {'zm_1'}, use_global_device_ids=true, to_apply=%region_39.40 | all-reduce | flops 1 | bytes 8 | tf_op jit(solution)/shard_map/psum | solution.py:24
  404.3 6.9 %psum.126 = f32[]{:T(128)} all-reduce(f32[]{:T(128)} %psum.125), channel_id=1, replica_groups=mesh['zm_0'=4,'zm_1'=4,'zv_0'=4,'zv_1'=2] {'zv_0'}, use_global_device_ids=true, to_apply=%region_40.41 | all-reduce | flops 1 | bytes 8 | tf_op jit(solution)/shard_map/psum | solution.py:24
  411.3 8.7 %psum.127 = f32[]{:T(128)} all-reduce(f32[]{:T(128)} %psum.126), channel_id=1, replica_groups=mesh['zm_0'=4,'zm_1'=4,'zv_0'=4,'zv_1'=2] {'zv_1'}, use_global_device_ids=true, to_apply=%region_41.42 | all-reduce | flops 1 | bytes 8 | tf_op jit(solution)/shard_map/psum | solution.py:24
  439.2 7.1 %all-reduce.2 = (f32[]{:T(128)}, f32[]{:T(128)}, f32[]{:T(128)}, f32[]{:T(128)}) all-reduce(f32[]{:T(128)} %get-tuple-element.24, f32[]{:T(128)} %get-tuple-element.21, f32[]{:T(128)} %get-tuple-element.18, f32[]{:T(128)} %get-tuple-element.15), channel_id=1, replica_groups=mesh['zm_0'=4,'zm_1'=4,'zv_0'=4,'zv_1'=2] {'zm_0'}, use_global_device_ids=true, to_apply=%region_64.65 | all-reduce | flops 4 | bytes 32 | tf_op jit(solution)/shard_map/pmax | solution.py:28
  453.0 7.3 %all-reduce = (f32[]{:T(128)}, f32[]{:T(128)}, f32[]{:T(128)}, f32[]{:T(128)}) all-reduce(f32[]{:T(128)} %get-tuple-element.39, f32[]{:T(128)} %get-tuple-element.40, f32[]{:T(128)} %get-tuple-element.41, f32[]{:T(128)} %get-tuple-element.42), channel_id=1, replica_groups=mesh['zm_0'=4,'zm_1'=4,'zv_0'=4,'zv_1'=2] {'zv_0'}, use_global_device_ids=true, to_apply=%region_66.67 | all-reduce | flops 4 | bytes 32 | tf_op jit(solution)/shard_map/pmax | solution.py:28
  460.3 9.0 %all-reduce.3 = (f32[1]{0:T(128)}, f32[1]{0:T(128)}, f32[1]{0:T(128)}, f32[1]{0:T(128)}) all-reduce(f32[1]{0:T(128)} %bitcast.55, f32[1]{0:T(128)} %bitcast.54, f32[1]{0:T(128)} %bitcast.53, f32[1]{0:T(128)} %bitcast.52), channel_id=1, replica_groups=mesh['zm_0'=4,'zm_1'=4,'zv_0'=4,'zv_1'=2] {'zv_1'}, use_global_device_ids=true, to_apply=%region_67.68 | all-reduce | flops 4 | bytes 32 | tf_op jit(solution)/shard_map/pmax | solution.py:28
  (253 shorter events, 251.1 us)
Async XLA Ops:
  2.2 26.9 %collective-permute-start = (f32[1,64,256]{2,0,1:T(1,128)}, f32[1,64,256]{2,0,1:T(1,128)}, u32[]{:S(2)}, u32[]{:S(2)}) collective-permute-start(f32[1,64,256]{2,0,1:T(1,128)} %copy.127), channel_id=1, source_target_pairs={{8,0},{16,8},{24,16},{32,24},{40,32},{48,40},{56,48},{64,56},{72,6... | collective-permute-start | bytes 196616 | tf_op jit(solution)/shard_map/ppermute | solution.py:34
  12.9 13.6 %copy-start.2 = (f32[16,64,256]{2,1,0:T(8,128)S(1)}, f32[16,64,256]{2,1,0:T(8,128)}, u32[]{:S(2)}) copy-start(f32[16,64,256]{2,1,0:T(8,128)} %param.3) | copy-start | bytes 3145732
  12.9 51.3 %all-to-all-start = ((f32[16,1,16384]{2,1,0:T(1,128)}), f32[16,1,16384]{2,1,0:T(1,128)S(1)}, u32[]{:S(2)}, u32[]{:S(2)}) async-start(f32[16,1,16384]{2,1,0:T(1,128)} %copy.126), calls=%async_computation | async-start | bytes 2097152 | tf_op jit(solution)/shard_map/all_to_all | solution.py:124
  30.1 8.4 %collective-permute-start.1 = (f32[17,1,256]{2,1,0:T(1,128)S(1)}, f32[17,1,256]{2,1,0:T(1,128)S(1)}, u32[]{:S(2)}, u32[]{:S(2)}) collective-permute-start(f32[17,1,256]{2,1,0:T(1,128)S(1)} %copy.130), channel_id=1, source_target_pairs={{1,0},{2,1},{3,2},{4,3},{5,4},{6,5},{7,6},{9,8},{10,9},{11,10},{12... | collective-permute-start | bytes 52232 | tf_op jit(solution)/shard_map/ppermute | solution.py:34
  78.4 95.4 %all-to-all-start.1 = ((f32[16,1,16384]{2,1,0:T(1,128)}), f32[16,1,16384]{2,1,0:T(1,128)}, u32[]{:S(2)}, u32[]{:S(2)}) async-start(f32[16,1,16384]{2,1,0:T(1,128)} %copy.139), calls=%async_computation.1 | async-start | bytes 2097152 | tf_op jit(solution)/shard_map/all_to_all | solution.py:124
  136.6 5.0 %collective-permute-start.2 = (f32[1,64,256]{2,0,1:T(1,128)S(1)}, f32[1,64,256]{2,0,1:T(1,128)S(1)}, u32[]{:S(2)}, u32[]{:S(2)}) collective-permute-start(f32[1,64,256]{2,0,1:T(1,128)S(1)} %slice.268), channel_id=1, source_target_pairs={{8,0},{16,8},{24,16},{32,24},{40,32},{48,40},{56,48},{64,56},{72,6... | collective-permute-start | bytes 196616 | tf_op jit(solution)/shard_map/ppermute | solution.py:34
  141.7 6.3 %collective-permute-start.3 = (f32[17,1,256]{2,1,0:T(1,128)S(1)}, f32[17,1,256]{2,1,0:T(1,128)S(1)}, u32[]{:S(2)}, u32[]{:S(2)}) collective-permute-start(f32[17,1,256]{2,1,0:T(1,128)S(1)} %copy.140), channel_id=1, source_target_pairs={{1,0},{2,1},{3,2},{4,3},{5,4},{6,5},{7,6},{9,8},{10,9},{11,10},{12... | collective-permute-start | bytes 52232 | tf_op jit(solution)/shard_map/ppermute | solution.py:34
  171.2 9.5 %copy-start.35 = (pred[16]{0:T(512)(128)(4,1)S(1)}, pred[16]{0:T(512)(128)(4,1)}, u32[]{:S(2)}) copy-start(pred[16]{0:T(512)(128)(4,1)} %broadcast_compare_fusion.10) | copy-start | bytes 52
  173.8 105.0 %all-to-all-start.2 = ((f32[16,1,16384]{2,1,0:T(1,128)}), f32[16,1,16384]{2,1,0:T(1,128)}, u32[]{:S(2)}, u32[]{:S(2)}) async-start(f32[16,1,16384]{2,1,0:T(1,128)} %copy.148), calls=%async_computation.2 | async-start | bytes 2097152 | tf_op jit(solution)/shard_map/all_to_all | solution.py:124
  180.7 15.0 %copy-start.27 = (f32[16]{0:T(128)S(1)}, f32[16]{0:T(128)}, u32[]{:S(2)}) copy-start(f32[16]{0:T(128)} %get-tuple-element.28) | copy-start | bytes 196
  180.7 15.0 %copy-start.28 = (f32[16]{0:T(128)S(1)}, f32[16]{0:T(128)}, u32[]{:S(2)}) copy-start(f32[16]{0:T(128)} %get-tuple-element.81) | copy-start | bytes 196
  241.2 11.9 %copy-start = (f32[16,64,256]{2,0,1:T(8,128)}, f32[16,64,256]{2,0,1:T(8,128)S(1)}, u32[]{:S(2)}) copy-start(f32[16,64,256]{2,0,1:T(8,128)S(1)} %add.505) | copy-start | bytes 3145732
  241.2 9.1 %copy-start.15 = (s32[16]{0:T(128)S(1)}, s32[16]{0:T(128)}, u32[]{:S(2)}) copy-start(s32[16]{0:T(128)} %copy-done.14) | copy-start | bytes 196
  241.2 9.1 %copy-start.21 = (pred[16]{0:T(512)(128)(4,1)S(1)}, pred[16]{0:T(512)(128)(4,1)}, u32[]{:S(2)}) copy-start(pred[16]{0:T(512)(128)(4,1)} %copy-done.20) | copy-start | bytes 52
  241.2 9.1 %copy-start.26 = (pred[16]{0:T(512)(128)(4,1)S(1)}, pred[16]{0:T(512)(128)(4,1)}, u32[]{:S(2)}) copy-start(pred[16]{0:T(512)(128)(4,1)} %get-tuple-element.93) | copy-start | bytes 52
  241.3 5.1 %collective-permute-start.4 = (f32[1,64,256]{2,0,1:T(1,128)S(1)}, f32[1,64,256]{2,0,1:T(1,128)S(1)}, u32[]{:S(2)}, u32[]{:S(2)}) collective-permute-start(f32[1,64,256]{2,0,1:T(1,128)S(1)} %slice.281), channel_id=1, source_target_pairs={{8,0},{16,8},{24,16},{32,24},{40,32},{48,40},{56,48},{64,56},{72,6... | collective-permute-start | bytes 196616 | tf_op jit(solution)/shard_map/ppermute | solution.py:34
  246.6 6.5 %collective-permute-start.5 = (f32[17,1,256]{2,1,0:T(1,128)S(1)}, f32[17,1,256]{2,1,0:T(1,128)S(1)}, u32[]{:S(2)}, u32[]{:S(2)}) collective-permute-start(f32[17,1,256]{2,1,0:T(1,128)S(1)} %copy.149), channel_id=1, source_target_pairs={{1,0},{2,1},{3,2},{4,3},{5,4},{6,5},{7,6},{9,8},{10,9},{11,10},{12... | collective-permute-start | bytes 52232 | tf_op jit(solution)/shard_map/ppermute | solution.py:34
  290.7 91.0 %all-to-all-start.3 = ((f32[16,1,16384]{2,1,0:T(1,128)}), f32[16,1,16384]{2,1,0:T(1,128)}, u32[]{:S(2)}, u32[]{:S(2)}) async-start(f32[16,1,16384]{2,1,0:T(1,128)} %copy.157), calls=%async_computation.3 | async-start | bytes 2097152 | tf_op jit(solution)/shard_map/all_to_all | solution.py:124
  345.4 5.0 %collective-permute-start.6 = (f32[1,64,256]{2,0,1:T(1,128)S(1)}, f32[1,64,256]{2,0,1:T(1,128)S(1)}, u32[]{:S(2)}, u32[]{:S(2)}) collective-permute-start(f32[1,64,256]{2,0,1:T(1,128)S(1)} %slice.294), channel_id=1, source_target_pairs={{8,0},{16,8},{24,16},{32,24},{40,32},{48,40},{56,48},{64,56},{72,6... | collective-permute-start | bytes 196616 | tf_op jit(solution)/shard_map/ppermute | solution.py:34
  350.6 5.2 %collective-permute-start.7 = (f32[17,1,256]{2,1,0:T(1,128)S(1)}, f32[17,1,256]{2,1,0:T(1,128)S(1)}, u32[]{:S(2)}, u32[]{:S(2)}) collective-permute-start(f32[17,1,256]{2,1,0:T(1,128)S(1)} %copy.158), channel_id=1, source_target_pairs={{1,0},{2,1},{3,2},{4,3},{5,4},{6,5},{7,6},{9,8},{10,9},{11,10},{12... | collective-permute-start | bytes 52232 | tf_op jit(solution)/shard_map/ppermute | solution.py:34
  381.6 14.2 %copy-start.13 = (f32[16,1,16]{2,1,0:T(1,128)S(1)}, f32[16,1,16]{2,1,0:T(1,128)}, u32[]{:S(2)}) copy-start(f32[16,1,16]{2,1,0:T(1,128)} %copy-done.12) | copy-start | bytes 3076
  381.6 22.6 %copy-start.9 = (f32[16,1,16]{2,1,0:T(1,128)S(1)}, f32[16,1,16]{2,1,0:T(1,128)}, u32[]{:S(2)}) copy-start(f32[16,1,16]{2,1,0:T(1,128)} %copy-done.8) | copy-start | bytes 3076
  381.6 29.6 %copy-start.11 = (f32[16,1,16]{2,1,0:T(1,128)S(1)}, f32[16,1,16]{2,1,0:T(1,128)}, u32[]{:S(2)}) copy-start(f32[16,1,16]{2,1,0:T(1,128)} %copy-done.10) | copy-start | bytes 3076
  381.6 44.5 %copy-start.7 = (f32[16,1,16]{2,1,0:T(1,128)S(1)}, f32[16,1,16]{2,1,0:T(1,128)}, u32[]{:S(2)}) copy-start(f32[16,1,16]{2,1,0:T(1,128)} %copy-done.6) | copy-start | bytes 3076
  (24 other events, 109.3 us)
where the time goes:
time: 481 us; the launch traced here: 473 us
  blocking collectives  183 us (38%)
  local copies, waits for them, and re-layouts  133 us (28%)
  other arithmetic  90.3 us (19%)
  starting transfers between devices  43.9 us (9%)
  waiting for transfers between devices  9.71 us (2%)
  between operations  7.56 us (2%)
  matrix products  5.09 us (1%)
    psum x16, blocking collectives, one_axis_at_a_time(): return functools.reduce(lax.psum, axes, x)  153 us
    reshape x8, local copies, waits for them, and re-layouts, shards(): centre.reshape(BLOCK_Z, vary_blocks, BLOCK_V, prog_blocks, BLOCK_C * S)  55.9 us
    pmax x4, blocking collectives, over_axes(): return functools.reduce(lax.pmax, axes, x)  30 us
    all_to_all x4, starting transfers between devices, shards(): lax.all_to_all(packed, ZM, split_axis=0, concat_axis=0, tiled=True)  24.6 us
    reduce_max x4, other arithmetic, shards(): jnp.max(peak_error)  21.5 us
    ppermute x8, starting transfers between devices, shifted(): lax.ppermute(value, axis, [(source, source + steps) for source in range(f...  19.3 us
    reshape x8, local copies, waits for them, and re-layouts, shards(): table = table + change_view.reshape(table_depth, table_span, table_wide)  18.7 us
    reduce_sum x4, other arithmetic, shards(): jnp.sum(residual * residual)  18.4 us
  transfers between devices with their start and end apart: 12, of which 4 were waited for; matrix products, arithmetic and copies ran while one was open for 40% of the time, Pallas kernels for 0%

commit v1 on v0

v1 whole, which is shorter than its diff:
```python
import functools

import jax
import jax.numpy as jnp
from jax import lax
from jax.experimental import pallas as pl
from jax.experimental.pallas import tpu as pltpu
from jax.sharding import Mesh
from jax.sharding import PartitionSpec as P

ITERS = 4
Y, X, Z, C = "zm_0", "zm_1", "zv_0", "zv_1"
NAMES = (Y, X, Z, C)
ZM = (Y, X)
ZV = (Z, C)
BLK = 16
ROWS = 16
WIDE = 1024
META = 48
F32 = jnp.float32

ORDER = (
    (2, 2), (3, 2), (2, 3), (1, 2), (2, 1), (3, 1), (1, 3), (3, 3),
    (1, 1), (2, 0), (0, 2), (3, 0), (0, 3), (1, 0), (0, 1),
)
ZV_ORDER = ((2, 1), (2, 0), (1, 1), (3, 1), (1, 0), (3, 0), (0, 1))


def at(*steps):
    return tuple(
        lax.rem(lax.axis_index(name) + step + lax.axis_size(name), lax.axis_size(name))
        for name, step in zip(NAMES, steps, strict=True)
    )


def beside(zm_step, zv_step):
    zm = lax.rem(lax.axis_index(Y) * 4 + lax.axis_index(X) + zm_step + 16, 16)
    zv = lax.rem(lax.axis_index(Z) * 2 + lax.axis_index(C) + zv_step + 8, 8)
    return (zm // 4, lax.rem(zm, 4), zv // 2, lax.rem(zv, 2))


def send(src, dst, send_sem, recv_sem, device):
    copy = pltpu.make_async_remote_copy(
        src_ref=src,
        dst_ref=dst,
        send_sem=send_sem,
        recv_sem=recv_sem,
        device_id=device,
        device_id_type=pl.DeviceIdType.MESH,
    )
    copy.start()
    return copy


def lanes(shape):
    return lax.broadcasted_iota(jnp.int32, shape, len(shape) - 1)


def kernel(
    meta,
    table_hbm,
    refined_hbm,
    out_hbm,
    error_ref,
    worst_ref,
    tab,
    ref0,
    ref1,
    ref2,
    ref3,
    got0,
    got1,
    got2,
    got3,
    stage,
    ext,
    res,
    mid,
    sums,
    peak,
    flat,
    hz_out,
    hz_in,
    hv_out,
    hv_in,
    hc_out,
    hc_in,
    zv_out,
    zv_in,
    zm_out,
    zm_in,
    in_sem,
    out_sem,
    bulk_send,
    bulk_recv,
    halo_send,
    halo_recv,
    sum_send,
    sum_recv,
):
    ref, got = (ref0, ref1, ref2, ref3), (got0, got1, got2, got3)
    zm_here = lax.axis_index(Y) * 4 + lax.axis_index(X)
    zv_here = lax.axis_index(Z) * 2 + lax.axis_index(C)
    zm_last = zm_here == 15
    zv_last = zv_here == 7
    half = lanes((ROWS, 128)) < 64
    half_row = lanes((1, 128)) < 64
    tail = lax.rem(lanes((ROWS, 128)), 64) >= 56

    loads = [
        pltpu.make_async_copy(refined_hbm.at[t], ref[t], in_sem.at[t])
        for t in range(ITERS)
    ]
    halves = [
        pltpu.make_async_copy(
            table_hbm.at[:, pl.ds(h * 128, 128)], tab.at[h], in_sem.at[ITERS + h]
        )
        for h in range(2)
    ]
    loads[0].start()
    for load in halves:
        load.start()
    for load in loads[1:]:
        load.start()

    barrier = pltpu.get_barrier_semaphore()
    partners = [at(y, x, 0, 0) for y, x in ORDER] + [at(0, 0, z, c) for z, c in ZV_ORDER]
    partners += [beside(1, 1), beside(-1, -1)]
    for partner in partners:
        pl.semaphore_signal(
            barrier, inc=1, device_id=partner, device_id_type=pl.DeviceIdType.MESH
        )

    def order_blocks(t):
        def one(j, _):
            stage[t, j] = ref[t][meta[t, j]]
            return 0

        lax.fori_loop(1, BLK, one, 0)
        got[t][0] = ref[t][meta[t, 0]]

    def send_blocks(t):
        copies = []
        for y, x in ORDER:
            j = y * 4 + x
            copies.append(
                send(stage.at[t, j], got[t].at[j], bulk_send.at[t, j], bulk_recv.at[t, j], at(y, x, 0, 0))
            )
        return copies

    def table_to_blocks():
        def one(bv, _):
            for q in range(8):
                for h in range(2):
                    even = tab[h, pl.ds(bv * 16 + 2 * q, ROWS, stride=64), :]
                    odd = tab[h, pl.ds(bv * 16 + 2 * q + 1, ROWS, stride=64), :]
                    ext[bv * 4 + 2 * h, 0:ROWS, q * 128 : (q + 1) * 128] = jnp.where(
                        half, even, pltpu.roll(odd, 64, 1)
                    )
                    ext[bv * 4 + 2 * h + 1, 0:ROWS, q * 128 : (q + 1) * 128] = jnp.where(
                        half, pltpu.roll(even, 64, 1), odd
                    )
            return 0

        lax.fori_loop(0, 4, one, 0)

    def blocks_to_table(src, dst):
        def one(bv, _):
            for q in range(8):
                for h in range(2):
                    low = src[bv * 4 + 2 * h, 0:ROWS, q * 128 : (q + 1) * 128]
                    high = src[bv * 4 + 2 * h + 1, 0:ROWS, q * 128 : (q + 1) * 128]
                    dst[h, pl.ds(bv * 16 + 2 * q, ROWS, stride=64), :] = jnp.where(
                        half, low, pltpu.roll(high, 64, 1)
                    )
                    dst[h, pl.ds(bv * 16 + 2 * q + 1, ROWS, stride=64), :] = jnp.where(
                        half, pltpu.roll(low, 64, 1), high
                    )
            return 0

        lax.fori_loop(0, 4, one, 0)

    def send_halos(src, e):
        for l in range(BLK):
            hz_out[e, l : l + 1, :] = src[l, 0:1, :]
        for b in range(4):
            hv_out[e, b] = src[b, 0:ROWS, 0:128]
            hc_out[e, b : b + 1, :] = src[b, 0:1, 0:128]
        return [
            send(hz_out.at[e], hz_in.at[e], halo_send.at[e, 0], halo_recv.at[e, 0], beside(-1, 0)),
            send(hv_out.at[e], hv_in.at[e], halo_send.at[e, 1], halo_recv.at[e, 1], beside(0, -1)),
            send(hc_out.at[e], hc_in.at[e], halo_send.at[e, 2], halo_recv.at[e, 2], beside(-1, -1)),
        ]

    def place_halos(dst, e):
        for l in range(BLK):
            dst[l, 16:17, :] = jnp.where(zm_last, dst[l, 15:16, :], hz_in[e, l : l + 1, :])
        for b in range(4):
            own = pltpu.roll(dst[12 + b, 0:ROWS, 896:1024], 64, 1)
            dst[16 + b, 0:ROWS, 0:128] = jnp.where(zv_last, own, hv_in[e, b])
            own_row = pltpu.roll(dst[12 + b, 16:17, 896:1024], 64, 1)
            next_row = jnp.where(zm_last, hv_in[e, b, 15:16, :], hc_in[e, b : b + 1, :])
            dst[16 + b, 16:17, 0:128] = jnp.where(zv_last, own_row, next_row)

    def advance(weight):
        def one(l, _):
            ext[l, 0:ROWS, :] = ext[l, 0:ROWS, :] + weight * res[l, 0:ROWS, :]
            ext[l, 16:17, :] = ext[l, 16:17, :] + weight * res[l, 16:17, :]
            return 0

        lax.fori_loop(0, BLK, one, 0)
        for b in range(16, 20):
            ext[b, 0:ROWS, 0:128] = ext[b, 0:ROWS, 0:128] + weight * res[b, 0:ROWS, 0:128]
            ext[b, 16:17, 0:128] = ext[b, 16:17, 0:128] + weight * res[b, 16:17, 0:128]

    def interpolate():
        def along_z(l, _):
            sums[l] = ext[l, 0:ROWS, :] + ext[l, 1 : ROWS + 1, :]
            return 0

        lax.fori_loop(0, BLK, along_z, 0)
        for b in range(16, 20):
            sums[b, :, 0:128] = ext[b, 0:ROWS, 0:128] + ext[b, 1 : ROWS + 1, 0:128]

        def along_v(l, _):
            for q in range(8):
                here = sums[l, :, q * 128 : (q + 1) * 128]
                if q < 7:
                    later = sums[l, :, (q + 1) * 128 : (q + 2) * 128]
                else:
                    later = sums[l + 4, :, 0:128]
                mid[l, :, q * 128 : (q + 1) * 128] = here + pltpu.roll(
                    jnp.where(half, later, here), 64, 1
                )
            return 0

        lax.fori_loop(0, BLK, along_v, 0)

        def along_c(bv, _):
            for b in range(4):
                l = bv * 4 + b
                for q in range(8):
                    here = mid[l, :, q * 128 : (q + 1) * 128]
                    if b < 3:
                        later = pltpu.roll(mid[l + 1, :, q * 128 : (q + 1) * 128], 56, 1)
                    else:
                        later = here
                    total = here + jnp.where(tail, later, pltpu.roll(here, 120, 1))
                    sums[l, :, q * 128 : (q + 1) * 128] = total * 0.125
            return 0

        lax.fori_loop(0, 4, along_c, 0)

    def residuals(t):
        def one(l, acc):
            j = meta[t, 16 + l]
            value = got[t][jnp.maximum(j, 0)] - sums[l]
            value = jnp.where(j >= 0, value, jnp.zeros_like(value))
            res[l, 0:ROWS, :] = value
            squares, largest = jnp.zeros((8, 128), F32), jnp.zeros((8, 128), F32)
            for r in range(2):
                for q in range(8):
                    part = value[r * 8 : (r + 1) * 8, q * 128 : (q + 1) * 128]
                    squares = squares + part * part
                    largest = jnp.maximum(largest, jnp.abs(part))
            peak[t, l] = largest
            return acc + squares

        acc = lax.fori_loop(0, BLK, one, jnp.zeros((8, 128), F32))
        return jnp.sum(acc, axis=0, keepdims=True)

    row_id = lax.broadcasted_iota(jnp.int32, (8, 128), 0)

    def join(a, b):
        return jnp.where(row_id == 0, a + b, jnp.maximum(a, b))

    def gather_zv(t):
        return [
            send(zv_out.at[t], zv_in.at[t, i], sum_send.at[t, i], sum_recv.at[t, i], at(0, 0, z, c))
            for i, (z, c) in enumerate(ZV_ORDER)
        ]

    def gather_zm(t):
        return [
            send(zm_out.at[t], zm_in.at[t, i], sum_send.at[t, 7 + i], sum_recv.at[t, 7 + i], at(y, x, 0, 0))
            for i, (y, x) in enumerate(ORDER)
        ]

    def weight_of(total, t):
        whole = jnp.sum(total, axis=1, keepdims=True)
        count = jnp.full((1, 1), meta[t, 32].astype(F32) * float(ROWS * WIDE))
        return 1.0 / (1.0 + jnp.sqrt(whole / count))

    pending = []
    loads[0].wait()
    order_blocks(0)
    for load in halves:
        load.wait()
    table_to_blocks()
    for t in range(1, ITERS):
        loads[t].wait()
        order_blocks(t)
    pl.semaphore_wait(barrier, len(partners))

    halos = send_halos(ext, 0)
    bulk = {0: send_blocks(0), 1: send_blocks(1)}
    for copy in halos:
        copy.wait_recv()
    pending += halos
    place_halos(ext, 0)

    for t in range(ITERS):
        interpolate()
        for copy in bulk[t]:
            copy.wait_recv()
        squares = residuals(t)
        zv_out[t, 0:1, :] = squares
        if t == ITERS - 1:
            for s in range(ITERS):
                largest = jnp.max(jnp.max(peak[s], axis=0), axis=0, keepdims=True)
                zv_out[t, s + 1 : s + 2, :] = largest
            zv_out[t, 5:8, :] = jnp.zeros((3, 128), F32)
        else:
            zv_out[t, 1:8, :] = jnp.zeros((7, 128), F32)
        first = gather_zv(t)
        if t < ITERS - 1:
            halos = send_halos(res, t + 1)
        else:
            blocks_to_table(ext, tab)
        for copy in first:
            copy.wait_recv()
        total = zv_out[t]
        for i in range(7):
            total = join(total, zv_in[t, i])
        zm_out[t] = total
        second = gather_zm(t)
        if t + 2 < ITERS:
            bulk[t + 2] = send_blocks(t + 2)
        if t == ITERS - 1:
            blocks_to_table(res, flat)
            for s in range(ITERS):
                lane_max = jnp.max(jnp.max(peak[s], axis=1), axis=1, keepdims=True)
                eye = lax.broadcasted_iota(jnp.int32, (BLK, BLK), 0) == lanes((BLK, BLK))
                spread = jnp.where(eye, jnp.broadcast_to(lane_max, (BLK, BLK)), 0.0)
                error_ref[s : s + 1, :] = jnp.max(spread, axis=0, keepdims=True)
        for copy in second:
            copy.wait_recv()
        for i in range(15):
            total = join(total, zm_in[t, i])
        weight = weight_of(total[0:1, :], t)
        pending += first + second
        if t < ITERS - 1:
            for copy in halos:
                copy.wait_recv()
            pending += halos
            place_halos(res, t + 1)
            advance(weight)

    stores = []
    for i in range(4):
        h, rows = i % 2, pl.ds(i // 2 * 512, 512)
        tab[h, rows, :] = tab[h, rows, :] + weight * flat[h, rows, :]
        store = pltpu.make_async_copy(
            tab.at[h, rows], out_hbm.at[rows, pl.ds(h * 128, 128)], out_sem.at[i]
        )
        store.start()
        stores.append(store)
    lane_max = jnp.max(total[1:5, :], axis=1, keepdims=True)
    worst_ref[...] = jnp.broadcast_to(lane_max, (4, 128))
    for t in range(ITERS):
        pending += bulk[t]
    for copy in pending:
        copy.wait_send()
    for store in stores:
        store.wait()


def shards(table, refined, assign):
    zm_here = lax.axis_index(ZM)
    zv_here = lax.axis_index(ZV)
    me_y, me_x = zm_here // 4, zm_here % 4
    device = zm_here * 8 + zv_here
    span = jnp.arange(16, dtype=jnp.int32)
    column = lax.dynamic_index_in_dim(assign.reshape(ITERS, 16, 8, 16), zv_here, 2, False)
    mine = jnp.sum(jnp.where((span == zm_here)[None, :, None], column, 0), axis=1)
    home = mine >> 7
    partner = ((me_y + span // 4) % 4) * 4 + (me_x + span % 4) % 4
    slots = jnp.sum(
        jnp.where(home[:, None, :] == partner[None, :, None], span[None, None, :], 0), axis=2
    )
    offset = ((me_y - span // 4) % 4) * 4 + (me_x - span % 4) % 4
    held = column[:, :, :, None] == device * BLK + span
    source = jnp.max(jnp.where(held, offset[None, :, None, None], -1), axis=(1, 2))
    count = jnp.sum((assign >= 0).astype(jnp.int32), axis=(1, 2))
    meta = jnp.concatenate(
        [slots, source, jnp.broadcast_to(count[:, None], (ITERS, META - 32))], axis=1
    )

    depth, width, chan = table.shape
    any_space = pl.BlockSpec(memory_space=pl.ANY)
    vmem = pl.BlockSpec(memory_space=pltpu.VMEM)
    dma = pltpu.SemaphoreType.DMA
    flat_table = (depth * width, chan)
    table_out, errors, worst = pl.pallas_call(
        kernel,
        out_shape=(
            jax.ShapeDtypeStruct(flat_table, F32),
            jax.ShapeDtypeStruct((ITERS, BLK), F32),
            jax.ShapeDtypeStruct((ITERS, 128), F32),
        ),
        in_specs=[pl.BlockSpec(memory_space=pltpu.SMEM), any_space, any_space],
        out_specs=(any_space, vmem, vmem),
        scratch_shapes=[
            pltpu.VMEM((2, depth * width, 128), F32),
            *[pltpu.VMEM((BLK, ROWS, WIDE), F32)] * (2 * ITERS),
            pltpu.VMEM((ITERS, BLK, ROWS, WIDE), F32),
            pltpu.VMEM((20, 24, WIDE), F32),
            pltpu.VMEM((20, 24, WIDE), F32),
            pltpu.VMEM((BLK, ROWS, WIDE), F32),
            pltpu.VMEM((20, ROWS, WIDE), F32),
            pltpu.VMEM((ITERS, BLK, 8, 128), F32),
            pltpu.VMEM((2, depth * width, 128), F32),
            pltpu.VMEM((ITERS, BLK, WIDE), F32),
            pltpu.VMEM((ITERS, BLK, WIDE), F32),
            pltpu.VMEM((ITERS, 4, ROWS, 128), F32),
            pltpu.VMEM((ITERS, 4, ROWS, 128), F32),
            pltpu.VMEM((ITERS, 8, 128), F32),
            pltpu.VMEM((ITERS, 8, 128), F32),
            pltpu.VMEM((ITERS, 8, 128), F32),
            pltpu.VMEM((ITERS, 7, 8, 128), F32),
            pltpu.VMEM((ITERS, 8, 128), F32),
            pltpu.VMEM((ITERS, 15, 8, 128), F32),
            dma((ITERS + 2,)),
            dma((4,)),
            dma((ITERS, BLK)),
            dma((ITERS, BLK)),
            dma((ITERS, 3)),
            dma((ITERS, 3)),
            dma((ITERS, 22)),
            dma((ITERS, 22)),
        ],
        compiler_params=pltpu.CompilerParams(collective_id=0, has_side_effects=True),
        name="refine",
    )(meta, table.reshape(flat_table), refined)
    return table_out.reshape(table.shape), errors, worst[:, 0]


def solution(mesh):
    split = Mesh(mesh.devices.reshape(4, 4, 4, 2), NAMES)
    in_specs = (P(ZM, ZV, None), P(None, NAMES, None, None), P())
    out_specs = (P(ZM, ZV, None), P(None, NAMES), P())
    return jax.shard_map(
        shards, mesh=split, in_specs=in_specs, out_specs=out_specs, check_vma=False
    )
```

time: 481 us -> 98.8 us (0.21); the launches traced: 473 us -> 98.4 us
  blocking collectives: 183 us -> 0 us
  local copies, waits for them, and re-layouts: 133 us -> 5.84 us
  Pallas kernels: 0 us -> 89.7 us
  other arithmetic: 90.3 us -> 2.16 us
  starting transfers between devices: 43.9 us -> 0 us
  waiting for transfers between devices: 9.71 us -> 0 us
  between operations: 7.56 us -> 0.71 us
  matrix products: 5.09 us -> 0 us
    psum x16 -> x0, blocking collectives: 153 us -> none  [one_axis_at_a_time(): return functools.reduce(lax.psum, axes, x)]
    reshape x24 -> x0, local copies, waits for them, and re-layouts: 94 us -> none  [the longest x8 55.9 us: shards(): centre.reshape(BLOCK_Z, vary_blocks, BLOCK_V, prog_blocks, BLOCK_C * S)]
    pallas_call x0 -> x1, Pallas kernels: none -> 89.7 us  [shards(): pl.pallas_call(kernel, out_shape=(jax.ShapeDtypeStruct(flat_table, F32),...]
    pmax x4 -> x0, blocking collectives: 30 us -> none  [over_axes(): return functools.reduce(lax.pmax, axes, x)]
    all_to_all x4 -> x0, starting transfers between devices: 24.6 us -> none  [shards(): lax.all_to_all(packed, ZM, split_axis=0, concat_axis=0, tiled=True)]
    reduce_sum x13 -> x3, other arithmetic: 22.5 us -> 1.22 us  [the longest x1 0.92 us: shards(): count = jnp.sum((assign >= 0).astype(jnp.int32), axis=(1, 2))]
    reduce_max x4 -> x1, other arithmetic: 21.5 us -> 0.23 us  [shards(): jnp.max(jnp.where(held, offset[None, :, None, None], -1), axis=(1, 2))]
    ppermute x8 -> x0, starting transfers between devices: 19.3 us -> none  [shifted(): lax.ppermute(value, axis, [(source, source + steps) for source in range(f...]
  transfers between devices with their start and end apart: 12 -> 0, of which waited for: 4 -> 0; matrix products, arithmetic and copies ran while one was open for 40% -> 0% of each run, Pallas kernels for 0% -> 0%
where the time goes in v1:
time: 98.8 us; the launch traced here: 98.4 us
  Pallas kernels  89.7 us (91%)
  local copies, waits for them, and re-layouts  5.84 us (6%)
  other arithmetic  2.16 us (2%)
    pallas_call x1, Pallas kernels, shards(): pl.pallas_call(kernel, out_shape=(jax.ShapeDtypeStruct(flat_table, F32),...  89.7 us
    unnamed x3, local copies, waits for them, and re-layouts  4.43 us

profile of v1, /device:TPU:1, one launch (start us, length us, event | category | flops | bytes accessed | tf_op | source)
XLA Modules:
  0.0 98.4 jit_solution(9846397653208497119)
XLA Ops:
  0.7 0.9 convert_reduce_fusion
  1.6 0.1 broadcast_in_dim.52
  1.7 0.9 copy.8
  2.6 0.2 select_reduce_fusion
  2.9 0.1 select_reduce_fusion.2
  3.0 0.2 select_reduce_fusion.1
  3.2 0.7 pad_add_fusion.meta
  3.8 89.7 %refine.1 = (f32[1024,256]{1,0:T(8,128)}, f32[4,16]{1,0:T(4,128)}, f32[4,128]{1,0:T(4,128)}) custom-call(s32[4,48]{1,0:T(4,128)} %pad_add_fusion.meta, f32[1024,256]{1,0:T(8,128)} %bitcast.4, f32[4,16,16,1024]{3,2,1,0:T(8,128)} %refined_hbm.1), custom_call_target="tpu_custom_call" | custom-call | tf_op jit(solution)/shard_map/refine/pallas_call | solution.py:404
  93.5 1.3 %slice_reduce_fusion = f32[4]{0:T(128)} fusion(f32[4,128]{1,0:T(4,128)} %get-tuple-element.8), kind=kLoop, calls=%fused_computation.13 | loop fusion | bytes 32 | tf_op jit(solution)/shard_map/slice | solution.py:445
  94.9 2.3 %copy.11 = f32[16,64,256]{2,1,0:T(8,128)} copy(f32[16,64,256]{2,1,0:T(8,128)} %bitcast.5) | data formatting | bytes 2097152
  97.1 1.3 %copy.12 = f32[4,16]{1,0:T(4,128)} copy(f32[4,16]{1,0:T(4,128)} %get-tuple-element.15) | data formatting | bytes 512
  (5 shorter events, 0.1 us)

commit v2 on v1

v2 whole, which is shorter than its diff:
```python
import functools

import jax
import jax.numpy as jnp
from jax import lax
from jax.experimental import pallas as pl
from jax.experimental.pallas import tpu as pltpu
from jax.sharding import Mesh
from jax.sharding import PartitionSpec as P

ITERS = 4
Y, X, Z, C = "zm_0", "zm_1", "zv_0", "zv_1"
NAMES = (Y, X, Z, C)
ZM = (Y, X)
ZV = (Z, C)
BLK = 16
ROWS = 16
WIDE = 1024
LEAD = 8
F32 = jnp.float32

ORDER = (
    (2, 2), (3, 2), (2, 3), (1, 2), (2, 1), (3, 1), (1, 3), (3, 3),
    (1, 1), (2, 0), (0, 2), (3, 0), (0, 3), (1, 0), (0, 1),
)
ZV_ORDER = ((2, 1), (2, 0), (1, 1), (3, 1), (1, 0), (3, 0), (0, 1))


def at(*steps):
    return tuple(
        lax.rem(lax.axis_index(name) + step + lax.axis_size(name), lax.axis_size(name))
        for name, step in zip(NAMES, steps, strict=True)
    )


def beside(zm_step, zv_step):
    zm = lax.rem(lax.axis_index(Y) * 4 + lax.axis_index(X) + zm_step + 16, 16)
    zv = lax.rem(lax.axis_index(Z) * 2 + lax.axis_index(C) + zv_step + 8, 8)
    return (zm // 4, lax.rem(zm, 4), zv // 2, lax.rem(zv, 2))


def send(src, dst, send_sem, recv_sem, device):
    copy = pltpu.make_async_remote_copy(
        src_ref=src,
        dst_ref=dst,
        send_sem=send_sem,
        recv_sem=recv_sem,
        device_id=device,
        device_id_type=pl.DeviceIdType.MESH,
    )
    copy.start()
    return copy


def both_ends(ref, send_sem, recv_sem):
    return pltpu.make_async_remote_copy(
        src_ref=ref,
        dst_ref=ref,
        send_sem=send_sem,
        recv_sem=recv_sem,
        device_id=at(0, 0, 0, 1),
        device_id_type=pl.DeviceIdType.MESH,
    )


def within(index):
    return jnp.minimum(jnp.maximum(index, 0), BLK - 1)


def lanes(shape):
    return lax.broadcasted_iota(jnp.int32, shape, len(shape) - 1)


def kernel(
    assign_hbm,
    table_hbm,
    refined_hbm,
    tab,
    flat,
    stats_ref,
    error_ref,
    slots,
    plan,
    meta,
    ref0,
    ref1,
    ref2,
    ref3,
    got0,
    got1,
    got2,
    got3,
    stage,
    ext,
    res,
    mean,
    mean_res,
    peak,
    hz_out,
    hz_in,
    hv_out,
    hv_in,
    hc_out,
    hc_in,
    zv_out,
    zv_in,
    zm_out,
    zm_in,
    in_sem,
    bulk_send,
    bulk_recv,
    halo_send,
    halo_recv,
    sum_send,
    sum_recv,
):
    ref, got = (ref0, ref1, ref2, ref3), (got0, got1, got2, got3)
    zm_here = lax.axis_index(Y) * 4 + lax.axis_index(X)
    zv_here = lax.axis_index(Z) * 2 + lax.axis_index(C)
    zm_last = zm_here == 15
    zv_last = zv_here == 7
    half = lanes((ROWS, 128)) < 64
    half_row = lanes((1, 128)) < 64
    tail = lax.rem(lanes((ROWS, 128)), 64) >= 56

    loads = [
        pltpu.make_async_copy(refined_hbm.at[t], ref[t], in_sem.at[t])
        for t in range(ITERS)
    ]
    halves = [
        pltpu.make_async_copy(
            table_hbm.at[:, pl.ds(h * 128, 128)], tab.at[h, pl.ds(0, 1024)], in_sem.at[ITERS + h]
        )
        for h in range(2)
    ]
    slots_load = pltpu.make_async_copy(assign_hbm, slots, in_sem.at[ITERS + 2])
    plan_load = pltpu.make_async_copy(plan, meta, in_sem.at[ITERS + 3])
    slots_load.start()
    loads[0].start()
    for load in halves:
        load.start()
    for load in loads[1:]:
        load.start()

    barrier = pltpu.get_barrier_semaphore()
    partners = [at(y, x, 0, 0) for y, x in ORDER] + [at(0, 0, z, c) for z, c in ZV_ORDER]
    partners += [beside(1, 1), beside(-1, -1)]
    for partner in partners:
        pl.semaphore_signal(
            barrier, inc=1, device_id=partner, device_id_type=pl.DeviceIdType.MESH
        )

    def make_plan():
        me_y, me_x = lax.axis_index(Y), lax.axis_index(X)
        device = zm_here * 8 + zv_here
        lane, sub = lanes((BLK, 128)), lax.broadcasted_iota(jnp.int32, (BLK, 128), 0)
        offset = ((me_y - (lane >> 5)) & 3) * 4 + ((me_x - ((lane >> 3) & 3)) & 3)
        partner = ((me_y + (lane >> 2)) & 3) * 4 + ((me_x + (lane & 3)) & 3)
        for t in range(ITERS):
            block = slots[t]
            here = jnp.where((block >> 4) == device, (block & 15).astype(F32), -1.0)
            here = jnp.max(here, axis=0, keepdims=True)
            source = jnp.where(here == sub.astype(F32), offset.astype(F32), -1.0)
            source = jnp.max(source, axis=1, keepdims=True)
            source = jnp.max(jnp.where(lane == sub, source, -1.0), axis=0, keepdims=True)
            home = jnp.where(lane == device, (block >> 7).astype(F32), 0.0)
            home = jnp.sum(home, axis=1, keepdims=True)
            slot = jnp.where(home == partner.astype(F32), sub.astype(F32), 0.0)
            slot = jnp.max(slot, axis=0, keepdims=True)
            count = jnp.sum(jnp.where(block >= 0, 1.0, 0.0), axis=0, keepdims=True)
            count = jnp.sum(count, axis=1, keepdims=True)
            plan[t : t + 1, :] = slot.astype(jnp.int32)
            plan[4 + t : 5 + t, :] = jnp.where(lane[0:1] < 16, source, count).astype(jnp.int32)

    def order_blocks(t):
        def one(j, _):
            stage[t, j] = ref[t][within(meta[t, j])]
            return 0

        lax.fori_loop(1, BLK, one, 0)
        got[t][0] = ref[t][within(meta[t, 0])]

    def table_to_blocks():
        def one(bv, _):
            for q in range(8):
                for h in range(2):
                    even = tab[h, pl.ds(bv * 16 + 2 * q, ROWS, stride=64), :]
                    odd = tab[h, pl.ds(bv * 16 + 2 * q + 1, ROWS, stride=64), :]
                    ext[bv * 4 + 2 * h, 0:ROWS, q * 128 : (q + 1) * 128] = jnp.where(
                        half, even, pltpu.roll(odd, 64, 1)
                    )
                    ext[bv * 4 + 2 * h + 1, 0:ROWS, q * 128 : (q + 1) * 128] = jnp.where(
                        half, pltpu.roll(even, 64, 1), odd
                    )
            return 0

        lax.fori_loop(0, 4, one, 0)

    def blocks_to_table(src, dst):
        def one(bv, _):
            for q in range(8):
                for h in range(2):
                    low = src[bv * 4 + 2 * h, 0:ROWS, q * 128 : (q + 1) * 128]
                    high = src[bv * 4 + 2 * h + 1, 0:ROWS, q * 128 : (q + 1) * 128]
                    dst[h, pl.ds(bv * 16 + 2 * q, ROWS, stride=64), :] = jnp.where(
                        half, low, pltpu.roll(high, 64, 1)
                    )
                    dst[h, pl.ds(bv * 16 + 2 * q + 1, ROWS, stride=64), :] = jnp.where(
                        half, pltpu.roll(low, 64, 1), high
                    )
            return 0

        lax.fori_loop(0, 4, one, 0)

    def pack_table_halos():
        for h in range(2):
            first = tab[h, pl.ds(0, ROWS, stride=64), :]
            hv_out[0, 2 * h] = first
            hv_out[0, 2 * h + 1] = pltpu.roll(first, 64, 1)
            hc_out[0, 2 * h : 2 * h + 1, :] = first[0:1]
            hc_out[0, 2 * h + 1 : 2 * h + 2, :] = pltpu.roll(first[0:1], 64, 1)

    def send_sides(e):
        return [
            send(hv_out.at[e], hv_in.at[e], halo_send.at[e, 1], halo_recv.at[e, 1], beside(0, -1)),
            send(hc_out.at[e], hc_in.at[e], halo_send.at[e, 2], halo_recv.at[e, 2], beside(-1, -1)),
        ]

    def send_table_halos():
        for h in range(2):
            send(
                table_hbm.at[pl.ds(0, 64), pl.ds(h * 128, 128)],
                tab.at[h, pl.ds(1024, 64)],
                halo_send.at[0, 0],
                halo_recv.at[0, 0],
                beside(-1, 0),
            )
        rows = both_ends(hz_in.at[0], halo_send.at[0, 0], halo_recv.at[0, 0])
        return [rows, *send_sides(0)]

    def unpack_table_halos():
        def one(bv, _):
            for q in range(8):
                for h in range(2):
                    cols = slice(q * 128, (q + 1) * 128)
                    even = tab[h, pl.ds(1024 + bv * 16 + 2 * q, 1), :]
                    odd = tab[h, pl.ds(1024 + bv * 16 + 2 * q + 1, 1), :]
                    low = jnp.where(half_row, even, pltpu.roll(odd, 64, 1))
                    high = jnp.where(half_row, pltpu.roll(even, 64, 1), odd)
                    for side, row in ((2 * h, low), (2 * h + 1, high)):
                        own = ext[bv * 4 + side, 15:16, cols]
                        ext[bv * 4 + side, 16:17, cols] = jnp.where(zm_last, own, row)
            return 0

        lax.fori_loop(0, 4, one, 0)

    def send_halos(src, e):
        for l in range(BLK):
            hz_out[e, l : l + 1, :] = src[l, 0:1, :]
        for b in range(4):
            hv_out[e, b] = src[b, 0:ROWS, 0:128]
            hc_out[e, b : b + 1, :] = src[b, 0:1, 0:128]
        return [
            send(hz_out.at[e], hz_in.at[e], halo_send.at[e, 0], halo_recv.at[e, 0], beside(-1, 0)),
            *send_sides(e),
        ]

    def place_v(dst, e):
        for b in range(4):
            own = pltpu.roll(dst[12 + b, 0:ROWS, 896:1024], 64, 1)
            dst[16 + b, 0:ROWS, 0:128] = jnp.where(zv_last, own, hv_in[e, b])

    def place_z(dst, e):
        for l in range(BLK):
            dst[l, 16:17, :] = jnp.where(zm_last, dst[l, 15:16, :], hz_in[e, l : l + 1, :])

    def place_corner(dst, e):
        for b in range(4):
            own_row = pltpu.roll(dst[12 + b, 16:17, 896:1024], 64, 1)
            next_row = jnp.where(zm_last, hv_in[e, b, 15:16, :], hc_in[e, b : b + 1, :])
            dst[16 + b, 16:17, 0:128] = jnp.where(zv_last, own_row, next_row)

    def interpolate(src, dst, top):
        def one(bv, _):
            def pair(l, q):
                cols = slice(q * 128, (q + 1) * 128)
                return src[l, top : top + 8, cols] + src[l, top + 1 : top + 9, cols]

            here = [pair(bv * 4 + b, 0) for b in range(4)]
            for q in range(8):
                if q < 7:
                    later = [pair(bv * 4 + b, q + 1) for b in range(4)]
                else:
                    later = [pair(bv * 4 + 4 + b, 0) for b in range(4)]
                both = [
                    here[b] + pltpu.roll(jnp.where(half[0:8], later[b], here[b]), 64, 1)
                    for b in range(4)
                ]
                for b in range(4):
                    beyond = pltpu.roll(both[b + 1], 56, 1) if b < 3 else both[b]
                    total = both[b] + jnp.where(tail[0:8], beyond, pltpu.roll(both[b], 120, 1))
                    dst[bv * 4 + b, top : top + 8, q * 128 : (q + 1) * 128] = total * 0.125
                here = later
            return 0

        lax.fori_loop(0, 4, one, 0)

    def fold(value, op):
        parts = [
            value[r * 8 : (r + 1) * 8, q * 128 : (q + 1) * 128]
            for r in range(2)
            for q in range(8)
        ]
        while len(parts) > 1:
            parts = [op(x, y) for x, y in zip(parts[::2], parts[1::2], strict=True)]
        return parts[0]

    def pack(values):
        row = jnp.zeros((1, 128), F32)
        for i, value in enumerate(values):
            row = jnp.where(lanes((1, 128)) == i, value, row)
        return row

    def wanted_minus(t, l):
        j = meta[4 + t, l]
        value = got[t][within(j)] - mean[l]
        return j >= 0, jnp.where(j >= 0, value, jnp.zeros_like(value))

    def first_residuals():
        def one(l, acc):
            _, value = wanted_minus(0, l)
            res[l, 0:ROWS, :] = value
            peak[0, l] = fold(jnp.abs(value), jnp.maximum)
            return acc + fold(value * value, jnp.add)

        acc = lax.fori_loop(0, BLK, one, jnp.zeros((8, 128), F32))
        zm_out[0] = pack([jnp.sum(jnp.sum(acc, axis=0, keepdims=True), axis=1, keepdims=True)])

    def products(t):
        def one(l, acc):
            live, a = wanted_minus(t, l)
            b = mean_res[l]
            b = jnp.where(live, b, jnp.zeros_like(b))
            return (
                acc[0] + fold(a * a, jnp.add),
                acc[1] + fold(a * b, jnp.add),
                acc[2] + fold(b * b, jnp.add),
            )

        zero = jnp.zeros((8, 128), F32)
        sums = lax.fori_loop(0, BLK, one, (zero, zero, zero))
        zm_out[t] = pack(
            [jnp.sum(jnp.sum(acc, axis=0, keepdims=True), axis=1, keepdims=True) for acc in sums]
        )

    def residuals(t, weight):
        scale = jnp.broadcast_to(weight, (8, 128))
        zero = jnp.zeros((8, 128), F32)

        def one(l, _):
            j = meta[4 + t, l]
            live, row = j >= 0, within(j)
            largest = []
            for r in (slice(0, 8), slice(8, 16)):
                for q in range(8):
                    c = slice(q * 128, (q + 1) * 128)
                    ext[l, r, c] = ext[l, r, c] + scale * res[l, r, c]
                    moved = mean[l, r, c] + scale * mean_res[l, r, c]
                    value = jnp.where(live, got[t][row, r, c] - moved, zero)
                    if t < ITERS - 1:
                        mean[l, r, c] = moved
                    res[l, r, c] = value
                    largest.append(jnp.abs(value))
            while len(largest) > 1:
                largest = [jnp.maximum(x, y) for x, y in zip(largest[::2], largest[1::2], strict=True)]
            peak[t, l] = largest[0]
            return 0

        lax.fori_loop(0, BLK, one, 0)

    def gather_zv(src, dst, k):
        for i, (z, c) in enumerate(ZV_ORDER):
            send(src, dst.at[i], sum_send.at[k, 0], sum_recv.at[k, 0], at(0, 0, z, c))
        return both_ends(dst, sum_send.at[k, 0], sum_recv.at[k, 0])

    def gather_zm(src, dst, k):
        for i, (y, x) in enumerate(ORDER):
            send(src, dst.at[i], sum_send.at[k, 1], sum_recv.at[k, 1], at(y, x, 0, 0))
        return both_ends(dst, sum_send.at[k, 1], sum_recv.at[k, 1])

    def weight_of(sums, t, before):
        def entry(i):
            return jnp.sum(jnp.where(lanes((1, 128)) == i, sums, 0.0), axis=1, keepdims=True)

        total = entry(0)
        if t:
            total = total - before * (2.0 * entry(1) - before * entry(2))
            total = jnp.maximum(total, 0.0)
        count = jnp.full((1, 1), meta[4 + t, 16].astype(F32) * float(ROWS * WIDE))
        return 1.0 / (1.0 + jnp.sqrt(total / count))

    sent = []

    def bulk_to(stop):
        for n in range(len(sent), min(stop, ITERS * len(ORDER))):
            t, (y, x) = n // len(ORDER), ORDER[n % len(ORDER)]
            j = y * 4 + x
            send(stage.at[t, j], got[t].at[j], bulk_send.at[t], bulk_recv.at[t], at(y, x, 0, 0))
            sent.append(n)

    def bulk(t):
        return both_ends(got[t].at[pl.ds(1, BLK - 1)], bulk_send.at[t], bulk_recv.at[t])

    scope = jax.named_scope
    pending = []
    with scope("slots"):
        slots_load.wait()
    with scope("plan"):
        make_plan()
        plan_load.start()
    with scope("load"):
        for load in halves:
            load.wait()
        pack_table_halos()
    with scope("plan_wait"):
        plan_load.wait()
    with scope("load"):
        loads[0].wait()
    with scope("order"):
        order_blocks(0)
    with scope("barrier"):
        pl.semaphore_wait(barrier, len(partners))
    with scope("bulk_start"):
        halos = send_table_halos()
        pending += halos
        bulk_to(15)
    with scope("order"):
        loads[1].wait()
        order_blocks(1)
    with scope("bulk_start"):
        bulk_to(15 + LEAD)
    with scope("relayout"):
        table_to_blocks()
    with scope("order"):
        for t in range(2, ITERS):
            loads[t].wait()
            order_blocks(t)
    with scope("halo_wait"):
        halos[1].wait_recv()
    with scope("interp"):
        place_v(ext, 0)
        interpolate(ext, mean, 0)
    with scope("halo_wait"):
        halos[0].wait_recv()
        halos[2].wait_recv()
    with scope("interp"):
        unpack_table_halos()
        place_corner(ext, 0)
        interpolate(ext, mean, 8)
    weight = None
    for t in range(ITERS):
        with scope("bulk_wait"):
            bulk(t).wait_recv()
        with scope("products"):
            if t == 0:
                first_residuals()
            else:
                products(t)
        with scope("zm_start"):
            first = gather_zm(zm_out.at[t], zm_in.at[t], t)
            pending.append(first)
        if t:
            with scope("zv_wait"):
                second.wait_recv()
                sums = zv_out[t - 1] + jnp.sum(zv_in[t - 1], axis=0)
                weight = weight_of(sums, t - 1, weight)
            with scope("residual"):
                residuals(t, weight)
        if t < ITERS - 1:
            with scope("halo_out"):
                halos = send_halos(res, t + 1)
                pending += halos
            with scope("bulk_start"):
                bulk_to(t * 15 + 30 + LEAD)
            with scope("halo_wait"):
                halos[1].wait_recv()
            with scope("interp"):
                place_v(res, t + 1)
                interpolate(res, mean_res, 0)
        else:
            with scope("max_start"):
                maxima = [
                    jnp.max(jnp.max(jnp.max(peak[s], axis=0), axis=0, keepdims=True), axis=1, keepdims=True)
                    for s in range(ITERS)
                ]
                zm_out[ITERS] = pack(maxima)
                first_max = gather_zm(zm_out.at[ITERS], zm_in.at[ITERS], ITERS)
                pending.append(first_max)
            with scope("relayout"):
                blocks_to_table(ext, tab)
        with scope("zm_wait"):
            first.wait_recv()
        with scope("zv_start"):
            zv_out[t] = zm_out[t] + jnp.sum(zm_in[t], axis=0)
            second = gather_zv(zv_out.at[t], zv_in.at[t], t)
            pending.append(second)
        if t < ITERS - 1:
            with scope("halo_wait"):
                halos[0].wait_recv()
                halos[2].wait_recv()
            with scope("interp"):
                place_z(res, t + 1)
                place_corner(res, t + 1)
                interpolate(res, mean_res, 8)
    with scope("relayout"):
        blocks_to_table(res, flat)
    with scope("max_next"):
        first_max.wait_recv()
        zv_out[ITERS] = jnp.maximum(zm_out[ITERS], jnp.max(zm_in[ITERS], axis=0))
        second_max = gather_zv(zv_out.at[ITERS], zv_in.at[ITERS], ITERS)
        pending.append(second_max)
    with scope("errors"):
        for s in range(ITERS):
            lane_max = jnp.max(jnp.max(peak[s], axis=1), axis=1, keepdims=True)
            eye = lax.broadcasted_iota(jnp.int32, (BLK, BLK), 0) == lanes((BLK, BLK))
            spread = jnp.where(eye, jnp.broadcast_to(lane_max, (BLK, BLK)), 0.0)
            error_ref[s : s + 1, :] = jnp.max(spread, axis=0, keepdims=True)
    with scope("zv_wait"):
        second.wait_recv()
        sums = zv_out[ITERS - 1] + jnp.sum(zv_in[ITERS - 1], axis=0)
        weight = weight_of(sums, ITERS - 1, weight)
        stats_ref[0:1, :] = jnp.broadcast_to(weight, (1, 128))
    with scope("max_wait"):
        second_max.wait_recv()
        stats_ref[1:2, :] = jnp.maximum(zv_out[ITERS], jnp.max(zv_in[ITERS], axis=0))
        stats_ref[2:8, :] = jnp.zeros((6, 128), F32)
    with scope("drain"):
        for copy in pending + [bulk(t) for t in range(ITERS)]:
            copy.wait_send()


def finish(tab, flat, stats, errors, out_hbm, error_ref, worst_ref, out, out_sem):
    stores = []
    for i in range(8):
        h, rows = i % 2, pl.ds(i // 2 * 256, 256)
        out[h, rows, :] = tab[h, rows, :] + stats[0:1, :] * flat[h, rows, :]
        store = pltpu.make_async_copy(
            out.at[h, rows], out_hbm.at[rows, pl.ds(h * 128, 128)], out_sem.at[i]
        )
        store.start()
        stores.append(store)
    error_ref[...] = errors[...]
    worst_ref[...] = stats[1:2, 0:ITERS]
    for store in stores:
        store.wait()


def shards(table, refined, assign):
    depth, width, chan = table.shape
    flat_table = (depth * width, chan)
    any_space = pl.BlockSpec(memory_space=pl.ANY)
    vmem = pl.BlockSpec(memory_space=pltpu.VMEM)
    dma = pltpu.SemaphoreType.DMA
    halves = (2, depth * width + width, 128)
    blocks = (BLK, ROWS, WIDE)
    tab, flat, stats, errors = pl.pallas_call(
        kernel,
        out_shape=(
            pltpu.VMEM(halves, F32),
            pltpu.VMEM((2, depth * width, 128), F32),
            pltpu.VMEM((8, 128), F32),
            pltpu.VMEM((ITERS, BLK), F32),
        ),
        in_specs=[any_space] * 3,
        out_specs=(vmem,) * 4,
        scratch_shapes=[
            pltpu.VMEM((ITERS, BLK, 128), jnp.int32),
            pltpu.VMEM((8, 128), jnp.int32),
            pltpu.SMEM((8, 128), jnp.int32),
            *[pltpu.VMEM(blocks, F32)] * (2 * ITERS),
            pltpu.VMEM((ITERS, *blocks), F32),
            pltpu.VMEM((20, 24, WIDE), F32),
            pltpu.VMEM((20, 24, WIDE), F32),
            pltpu.VMEM(blocks, F32),
            pltpu.VMEM(blocks, F32),
            pltpu.VMEM((ITERS, BLK, 8, 128), F32),
            pltpu.VMEM((ITERS, BLK, WIDE), F32),
            pltpu.VMEM((ITERS, BLK, WIDE), F32),
            pltpu.VMEM((ITERS, 4, ROWS, 128), F32),
            pltpu.VMEM((ITERS, 4, ROWS, 128), F32),
            pltpu.VMEM((ITERS, 8, 128), F32),
            pltpu.VMEM((ITERS, 8, 128), F32),
            pltpu.VMEM((ITERS + 1, 1, 128), F32),
            pltpu.VMEM((ITERS + 1, 7, 1, 128), F32),
            pltpu.VMEM((ITERS + 1, 1, 128), F32),
            pltpu.VMEM((ITERS + 1, 15, 1, 128), F32),
            dma((ITERS + 4,)),
            dma((ITERS,)),
            dma((ITERS,)),
            dma((ITERS, 3)),
            dma((ITERS, 3)),
            dma((ITERS + 1, 2)),
            dma((ITERS + 1, 2)),
        ],
        compiler_params=pltpu.CompilerParams(collective_id=0, has_side_effects=True),
        name="refine",
    )(jnp.transpose(assign, (0, 2, 1)), table.reshape(flat_table), refined)
    held = [pltpu.with_memory_space_constraint(x, pltpu.VMEM) for x in (tab, flat, stats, errors)]
    table_out, errors, worst = pl.pallas_call(
        finish,
        out_shape=(
            jax.ShapeDtypeStruct(flat_table, F32),
            jax.ShapeDtypeStruct((ITERS, BLK), F32),
            jax.ShapeDtypeStruct((1, ITERS), F32),
        ),
        in_specs=[vmem] * 4,
        out_specs=(any_space, vmem, vmem),
        scratch_shapes=[pltpu.VMEM((2, depth * width, 128), F32), dma((8,))],
        name="finish",
    )(*held)
    return table_out.reshape(table.shape), errors, worst.reshape(ITERS)


def solution(mesh):
    split = Mesh(mesh.devices.reshape(4, 4, 4, 2), NAMES)
    in_specs = (P(ZM, ZV, None), P(None, NAMES, None, None), P())
    out_specs = (P(ZM, ZV, None), P(None, NAMES), P())
    return jax.shard_map(
        shards, mesh=split, in_specs=in_specs, out_specs=out_specs, check_vma=False
    )
```

time: 98.8 us -> 81 us (0.82)
  Pallas kernels: 89.7 us -> 80.2 us
  local copies, waits for them, and re-layouts: 5.84 us -> 0 us
  other arithmetic: 2.16 us -> 0 us
    pallas_call x1 -> x2, Pallas kernels: 89.7 us -> 80.2 us  [the longest x1 78.6 us: shards(): pl.pallas_call(kernel, out_shape=(pltpu.VMEM(halves, F32), pltpu.VMEM((2,...]
    unnamed x3 -> x0, local copies, waits for them, and re-layouts: 4.43 us -> none
    slice x1 -> x0, local copies, waits for them, and re-layouts: 1.31 us -> none  [shards(): return (table_out.reshape(table.shape), errors, worst[:, 0])]
    reduce_sum x3 -> x0, other arithmetic: 1.22 us -> none  [the longest x1 0.92 us: shards(): count = jnp.sum((assign >= 0).astype(jnp.int32), axis=(1, 2))]
where the time goes in v2:
time: 81 us; the launch traced here: 80.9 us
  Pallas kernels  80.2 us (99%)
    pallas_call x1, Pallas kernels, shards(): pl.pallas_call(kernel, out_shape=(pltpu.VMEM(halves, F32), pltpu.VMEM((2,...  78.6 us
    pallas_call x1, Pallas kernels, shards(): pl.pallas_call(finish, out_shape=(jax.ShapeDtypeStruct(flat_table, F32),...  1.62 us

profile of v2, /device:TPU:1, one launch (start us, length us, event | category | flops | bytes accessed | tf_op | source)
XLA Modules:
  0.0 80.9 jit_solution(3557202838945165911)
XLA Ops:
  0.6 78.6 %refine.1 = (f32[2,1088,128]{2,1,0:T(8,128)S(1)}, f32[2,1024,128]{2,1,0:T(8,128)S(1)}, f32[8,128]{1,0:T(8,128)S(1)}, f32[4,16]{1,0:T(4,128)S(1)}) custom-call(s32[4,16,128]{2,1,0:T(8,128)} %bitcast.5, f32[1024,256]{1,0:T(8,128)} %bitcast.4, f32[4,16,16,1024]{3,2,1,0:T(8,128)} %refined_hbm.1), custom_call_target="tpu_custom_call" | custom-call | tf_op jit(solution)/shard_map/refine/pallas_call | solution.py:566
  79.2 1.6 %finish.1 = (f32[1024,256]{1,0:T(8,128)}, f32[4,16]{1,0:T(4,128)}, f32[1,4]{1,0:T(1,128)}) custom-call(f32[2,1088,128]{2,1,0:T(8,128)S(1)} %get-tuple-element.10.tab, f32[2,1024,128]{2,1,0:T(8,128)S(1)} %get-tuple-element.11.flat, f32[8,128]{1,0:T(8,128)S(1)} %get-tuple-element.12.stats, f32[4,16]{1,0:T(4,128)S(1)} %get-tuple-element.13.errors), custom_call_target="tpu_custom_call" | custom-call | tf_op jit(solution)/shard_map/finish/pallas_call | solution.py:609

commit v3 on v2

--- a/solution.py
+++ b/solution.py
@@ -16,7 +16,7 @@
 BLK = 16
 ROWS = 16
 WIDE = 1024
-LEAD = 8
+LEAD = (4, 4, 4, 0)
 F32 = jnp.float32
 
 ORDER = (
@@ -24,6 +24,10 @@
     (1, 1), (2, 0), (0, 2), (3, 0), (0, 3), (1, 0), (0, 1),
 )
 ZV_ORDER = ((2, 1), (2, 0), (1, 1), (3, 1), (1, 0), (3, 0), (0, 1))
+OTHERS = sorted(
+    [(y, x, z, c) for y in range(4) for x in range(4) for z in range(4) for c in range(2)][1:],
+    key=lambda d: (-min(d[0], 4 - d[0]) - min(d[1], 4 - d[1]) - min(d[2], 4 - d[2]) - d[3] / 2, d),
+)
 
 
 def at(*steps):
@@ -102,10 +106,8 @@
     hv_in,
     hc_out,
     hc_in,
-    zv_out,
-    zv_in,
-    zm_out,
-    zm_in,
+    sum_out,
+    all_in,
     in_sem,
     bulk_send,
     bulk_recv,
@@ -113,6 +115,7 @@
     halo_recv,
     sum_send,
     sum_recv,
+    entered,
 ):
     ref, got = (ref0, ref1, ref2, ref3), (got0, got1, got2, got3)
     zm_here = lax.axis_index(Y) * 4 + lax.axis_index(X)
@@ -334,7 +337,7 @@
             return acc + fold(value * value, jnp.add)
 
         acc = lax.fori_loop(0, BLK, one, jnp.zeros((8, 128), F32))
-        zm_out[0] = pack([jnp.sum(jnp.sum(acc, axis=0, keepdims=True), axis=1, keepdims=True)])
+        sum_out[0] = pack([jnp.sum(jnp.sum(acc, axis=0, keepdims=True), axis=1, keepdims=True)])
 
     def products(t):
         def one(l, acc):
@@ -349,7 +352,7 @@
 
         zero = jnp.zeros((8, 128), F32)
         sums = lax.fori_loop(0, BLK, one, (zero, zero, zero))
-        zm_out[t] = pack(
+        sum_out[t] = pack(
             [jnp.sum(jnp.sum(acc, axis=0, keepdims=True), axis=1, keepdims=True) for acc in sums]
         )
 
@@ -357,10 +360,10 @@
         scale = jnp.broadcast_to(weight, (8, 128))
         zero = jnp.zeros((8, 128), F32)
 
-        def one(l, _):
+        def one(l, acc):
             j = meta[4 + t, l]
             live, row = j >= 0, within(j)
-            largest = []
+            largest, squares = [], []
             for r in (slice(0, 8), slice(8, 16)):
                 for q in range(8):
                     c = slice(q * 128, (q + 1) * 128)
@@ -371,29 +374,26 @@
                         mean[l, r, c] = moved
                     res[l, r, c] = value
                     largest.append(jnp.abs(value))
+                    squares.append(value * value)
             while len(largest) > 1:
                 largest = [jnp.maximum(x, y) for x, y in zip(largest[::2], largest[1::2], strict=True)]
+                squares = [x + y for x, y in zip(squares[::2], squares[1::2], strict=True)]
             peak[t, l] = largest[0]
-            return 0
-
-        lax.fori_loop(0, BLK, one, 0)
-
-    def gather_zv(src, dst, k):
-        for i, (z, c) in enumerate(ZV_ORDER):
-            send(src, dst.at[i], sum_send.at[k, 0], sum_recv.at[k, 0], at(0, 0, z, c))
-        return both_ends(dst, sum_send.at[k, 0], sum_recv.at[k, 0])
-
-    def gather_zm(src, dst, k):
-        for i, (y, x) in enumerate(ORDER):
-            send(src, dst.at[i], sum_send.at[k, 1], sum_recv.at[k, 1], at(y, x, 0, 0))
-        return both_ends(dst, sum_send.at[k, 1], sum_recv.at[k, 1])
+            return acc + squares[0] if t == ITERS - 1 else acc
+
+        return lax.fori_loop(0, BLK, one, zero)
+
+    def gather(t):
+        for i, steps in enumerate(OTHERS):
+            send(sum_out.at[t], all_in.at[t, i], sum_send.at[t], sum_recv.at[t], at(*steps))
+        return both_ends(all_in.at[t], sum_send.at[t], sum_recv.at[t])
 
     def weight_of(sums, t, before):
         def entry(i):
             return jnp.sum(jnp.where(lanes((1, 128)) == i, sums, 0.0), axis=1, keepdims=True)
 
         total = entry(0)
-        if t:
+        if before is not None:
             total = total - before * (2.0 * entry(1) - before * entry(2))
             total = jnp.maximum(total, 0.0)
         count = jnp.full((1, 1), meta[4 + t, 16].astype(F32) * float(ROWS * WIDE))
@@ -430,6 +430,10 @@
         order_blocks(0)
     with scope("barrier"):
         pl.semaphore_wait(barrier, len(partners))
+    for z, c in ZV_ORDER:
+        pl.semaphore_signal(
+            entered, inc=1, device_id=at(0, 0, z, c), device_id_type=pl.DeviceIdType.MESH
+        )
     with scope("bulk_start"):
         halos = send_table_halos()
         pending += halos
@@ -438,7 +442,7 @@
         loads[1].wait()
         order_blocks(1)
     with scope("bulk_start"):
-        bulk_to(15 + LEAD)
+        bulk_to(15 + LEAD[0])
     with scope("relayout"):
         table_to_blocks()
     with scope("order"):
@@ -457,8 +461,9 @@
         unpack_table_halos()
         place_corner(ext, 0)
         interpolate(ext, mean, 8)
+    pl.semaphore_wait(entered, len(ZV_ORDER))
     weight = None
-    for t in range(ITERS):
+    for t in range(ITERS - 1):
         with scope("bulk_wait"):
             bulk(t).wait_recv()
         with scope("products"):
@@ -466,77 +471,71 @@
                 first_residuals()
             else:
                 products(t)
-        with scope("zm_start"):
-            first = gather_zm(zm_out.at[t], zm_in.at[t], t)
-            pending.append(first)
+        with scope("sum_start"):
+            coming = gather(t)
+            pending.append(coming)
         if t:
-            with scope("zv_wait"):
-                second.wait_recv()
-                sums = zv_out[t - 1] + jnp.sum(zv_in[t - 1], axis=0)
-                weight = weight_of(sums, t - 1, weight)
+            with scope("sum_wait"):
+                gone.wait_recv()
+                weight = weight_of(sum_out[t - 1] + jnp.sum(all_in[t - 1], axis=0), t - 1, weight)
             with scope("residual"):
                 residuals(t, weight)
-        if t < ITERS - 1:
-            with scope("halo_out"):
-                halos = send_halos(res, t + 1)
-                pending += halos
-            with scope("bulk_start"):
-                bulk_to(t * 15 + 30 + LEAD)
-            with scope("halo_wait"):
-                halos[1].wait_recv()
-            with scope("interp"):
-                place_v(res, t + 1)
-                interpolate(res, mean_res, 0)
-        else:
-            with scope("max_start"):
-                maxima = [
-                    jnp.max(jnp.max(jnp.max(peak[s], axis=0), axis=0, keepdims=True), axis=1, keepdims=True)
-                    for s in range(ITERS)
-                ]
-                zm_out[ITERS] = pack(maxima)
-                first_max = gather_zm(zm_out.at[ITERS], zm_in.at[ITERS], ITERS)
-                pending.append(first_max)
-            with scope("relayout"):
-                blocks_to_table(ext, tab)
-        with scope("zm_wait"):
-            first.wait_recv()
-        with scope("zv_start"):
-            zv_out[t] = zm_out[t] + jnp.sum(zm_in[t], axis=0)
-            second = gather_zv(zv_out.at[t], zv_in.at[t], t)
-            pending.append(second)
-        if t < ITERS - 1:
-            with scope("halo_wait"):
-                halos[0].wait_recv()
-                halos[2].wait_recv()
-            with scope("interp"):
-                place_z(res, t + 1)
-                place_corner(res, t + 1)
-                interpolate(res, mean_res, 8)
+        gone = coming
+        with scope("halo_out"):
+            halos = send_halos(res, t + 1)
+            pending += halos
+        with scope("bulk_start"):
+            bulk_to(t * 15 + 30 + LEAD[t + 1])
+        with scope("halo_wait"):
+            halos[1].wait_recv()
+        with scope("interp"):
+            place_v(res, t + 1)
+            interpolate(res, mean_res, 0)
+        with scope("halo_wait"):
+            halos[0].wait_recv()
+            halos[2].wait_recv()
+        with scope("interp"):
+            place_z(res, t + 1)
+            place_corner(res, t + 1)
+            interpolate(res, mean_res, 8)
+
+    t = ITERS - 1
+    with scope("sum_wait"):
+        gone.wait_recv()
+        weight = weight_of(sum_out[t - 1] + jnp.sum(all_in[t - 1], axis=0), t - 1, weight)
+    with scope("bulk_wait"):
+        bulk(t).wait_recv()
+    with scope("residual"):
+        squares = residuals(t, weight)
+    with scope("sum_start"):
+        values = [jnp.sum(jnp.sum(squares, axis=0, keepdims=True), axis=1, keepdims=True)]
+        for s in range(ITERS):
+            largest = jnp.max(jnp.max(peak[s], axis=0), axis=0, keepdims=True)
+            values.append(jnp.max(largest, axis=1, keepdims=True))
+        sum_out[t] = pack(values)
+        gone = gather(t)
+        pending.append(gone)
     with scope("relayout"):
+        blocks_to_table(ext, tab)
         blocks_to_table(res, flat)
-    with scope("max_next"):
-        first_max.wait_recv()
-        zv_out[ITERS] = jnp.maximum(zm_out[ITERS], jnp.max(zm_in[ITERS], axis=0))
-        second_max = gather_zv(zv_out.at[ITERS], zv_in.at[ITERS], ITERS)
-        pending.append(second_max)
     with scope("errors"):
         for s in range(ITERS):
             lane_max = jnp.max(jnp.max(peak[s], axis=1), axis=1, keepdims=True)
             eye = lax.broadcasted_iota(jnp.int32, (BLK, BLK), 0) == lanes((BLK, BLK))
             spread = jnp.where(eye, jnp.broadcast_to(lane_max, (BLK, BLK)), 0.0)
             error_ref[s : s + 1, :] = jnp.max(spread, axis=0, keepdims=True)
-    with scope("zv_wait"):
-        second.wait_recv()
-        sums = zv_out[ITERS - 1] + jnp.sum(zv_in[ITERS - 1], axis=0)
-        weight = weight_of(sums, ITERS - 1, weight)
+    with scope("drain"):
+        for copy in pending[:-1] + [bulk(s) for s in range(ITERS)]:
+            copy.wait_send()
+    with scope("sum_wait"):
+        gone.wait_recv()
+        gone.wait_send()
+    with scope("final"):
+        sums = sum_out[t] + jnp.sum(all_in[t], axis=0)
+        weight = weight_of(sums, t, None)
         stats_ref[0:1, :] = jnp.broadcast_to(weight, (1, 128))
-    with scope("max_wait"):
-        second_max.wait_recv()
-        stats_ref[1:2, :] = jnp.maximum(zv_out[ITERS], jnp.max(zv_in[ITERS], axis=0))
+        stats_ref[1:2, :] = jnp.maximum(sum_out[t], jnp.max(all_in[t], axis=0))
         stats_ref[2:8, :] = jnp.zeros((6, 128), F32)
-    with scope("drain"):
-        for copy in pending + [bulk(t) for t in range(ITERS)]:
-            copy.wait_send()
 
 
 def finish(tab, flat, stats, errors, out_hbm, error_ref, worst_ref, out, out_sem):
@@ -550,7 +549,7 @@
         store.start()
         stores.append(store)
     error_ref[...] = errors[...]
-    worst_ref[...] = stats[1:2, 0:ITERS]
+    worst_ref[...] = stats[1:2, 1 : ITERS + 1]
     for store in stores:
         store.wait()
 
@@ -590,17 +589,16 @@
             pltpu.VMEM((ITERS, 4, ROWS, 128), F32),
             pltpu.VMEM((ITERS, 8, 128), F32),
             pltpu.VMEM((ITERS, 8, 128), F32),
-            pltpu.VMEM((ITERS + 1, 1, 128), F32),
-            pltpu.VMEM((ITERS + 1, 7, 1, 128), F32),
-            pltpu.VMEM((ITERS + 1, 1, 128), F32),
-            pltpu.VMEM((ITERS + 1, 15, 1, 128), F32),
+            pltpu.VMEM((ITERS, 1, 128), F32),
+            pltpu.VMEM((ITERS, len(OTHERS), 1, 128), F32),
             dma((ITERS + 4,)),
             dma((ITERS,)),
             dma((ITERS,)),
             dma((ITERS, 3)),
             dma((ITERS, 3)),
-            dma((ITERS + 1, 2)),
-            dma((ITERS + 1, 2)),
+            dma((ITERS,)),
+            dma((ITERS,)),
+            pltpu.SemaphoreType.REGULAR,
         ],
         compiler_params=pltpu.CompilerParams(collective_id=0, has_side_effects=True),
         name="refine",

time: 81 us -> 76.4 us (0.943)
  Pallas kernels: 80.2 us -> 75.7 us
    pallas_call x1, Pallas kernels: 78.6 us -> 74 us  [shards(): pl.pallas_call(kernel, out_shape=(pltpu.VMEM(halves, F32), pltpu.VMEM((2,...]
where the time goes in v3:
time: 76.4 us; the launch traced here: 76.3 us
  Pallas kernels  75.7 us (99%)
    pallas_call x1, Pallas kernels, shards(): pl.pallas_call(kernel, out_shape=(pltpu.VMEM(halves, F32), pltpu.VMEM((2,...  74 us
    pallas_call x1, Pallas kernels, shards(): pl.pallas_call(finish, out_shape=(jax.ShapeDtypeStruct(flat_table, F32),...  1.63 us

profile of v3, /device:TPU:1, one launch (start us, length us, event | category | flops | bytes accessed | tf_op | source)
XLA Modules:
  0.0 76.3 jit_solution(6881883889556955132)
XLA Ops:
  0.6 74.0 %refine.1 = (f32[2,1088,128]{2,1,0:T(8,128)S(1)}, f32[2,1024,128]{2,1,0:T(8,128)S(1)}, f32[8,128]{1,0:T(8,128)S(1)}, f32[4,16]{1,0:T(4,128)S(1)}) custom-call(s32[4,16,128]{2,1,0:T(8,128)} %bitcast.5, f32[1024,256]{1,0:T(8,128)} %bitcast.4, f32[4,16,16,1024]{3,2,1,0:T(8,128)} %refined_hbm.1), custom_call_target="tpu_custom_call" | custom-call | tf_op jit(solution)/shard_map/refine/pallas_call | solution.py:565
  74.7 1.6 %finish.1 = (f32[1024,256]{1,0:T(8,128)}, f32[4,16]{1,0:T(4,128)}, f32[1,4]{1,0:T(1,128)}) custom-call(f32[2,1088,128]{2,1,0:T(8,128)S(1)} %get-tuple-element.10.tab, f32[2,1024,128]{2,1,0:T(8,128)S(1)} %get-tuple-element.11.flat, f32[8,128]{1,0:T(8,128)S(1)} %get-tuple-element.12.stats, f32[4,16]{1,0:T(4,128)S(1)} %get-tuple-element.13.errors), custom_call_target="tpu_custom_call" | custom-call | tf_op jit(solution)/shard_map/finish/pallas_call | solution.py:607

commit v4 on v3

--- a/solution.py
+++ b/solution.py
@@ -16,7 +16,8 @@
 BLK = 16
 ROWS = 16
 WIDE = 1024
-LEAD = (4, 4, 4, 0)
+TWO_STAGES = (True, True, True, False)
+LEAD = (3, 3, 3, 0)
 F32 = jnp.float32
 
 ORDER = (
@@ -108,6 +109,9 @@
     hc_in,
     sum_out,
     all_in,
+    zm_in,
+    zv_out,
+    zv_in,
     in_sem,
     bulk_send,
     bulk_recv,
@@ -115,6 +119,8 @@
     halo_recv,
     sum_send,
     sum_recv,
+    line_send,
+    line_recv,
     entered,
 ):
     ref, got = (ref0, ref1, ref2, ref3), (got0, got1, got2, got3)
@@ -387,6 +393,21 @@
         for i, steps in enumerate(OTHERS):
             send(sum_out.at[t], all_in.at[t, i], sum_send.at[t], sum_recv.at[t], at(*steps))
         return both_ends(all_in.at[t], sum_send.at[t], sum_recv.at[t])
+
+    def gather_zm(t):
+        for i, (y, x) in enumerate(ORDER):
+            send(sum_out.at[t], zm_in.at[t, i], sum_send.at[t], sum_recv.at[t], at(y, x, 0, 0))
+        return both_ends(zm_in.at[t], sum_send.at[t], sum_recv.at[t])
+
+    def gather_zv(t):
+        for i, (z, c) in enumerate(ZV_ORDER):
+            send(zv_out.at[t], zv_in.at[t, i], line_send.at[t], line_recv.at[t], at(0, 0, z, c))
+        return both_ends(zv_in.at[t], line_send.at[t], line_recv.at[t])
+
+    def sums_of(t):
+        if TWO_STAGES[t]:
+            return zv_out[t] + jnp.sum(zv_in[t], axis=0)
+        return sum_out[t] + jnp.sum(all_in[t], axis=0)
 
     def weight_of(sums, t, before):
         def entry(i):
@@ -472,12 +493,12 @@
             else:
                 products(t)
         with scope("sum_start"):
-            coming = gather(t)
+            coming = gather_zm(t) if TWO_STAGES[t] else gather(t)
             pending.append(coming)
         if t:
             with scope("sum_wait"):
                 gone.wait_recv()
-                weight = weight_of(sum_out[t - 1] + jnp.sum(all_in[t - 1], axis=0), t - 1, weight)
+                weight = weight_of(sums_of(t - 1), t - 1, weight)
             with scope("residual"):
                 residuals(t, weight)
         gone = coming
@@ -491,6 +512,12 @@
         with scope("interp"):
             place_v(res, t + 1)
             interpolate(res, mean_res, 0)
+        if TWO_STAGES[t]:
+            with scope("zm_wait"):
+                gone.wait_recv()
+                zv_out[t] = sum_out[t] + jnp.sum(zm_in[t], axis=0)
+                gone = gather_zv(t)
+                pending.append(gone)
         with scope("halo_wait"):
             halos[0].wait_recv()
             halos[2].wait_recv()
@@ -502,7 +529,7 @@
     t = ITERS - 1
     with scope("sum_wait"):
         gone.wait_recv()
-        weight = weight_of(sum_out[t - 1] + jnp.sum(all_in[t - 1], axis=0), t - 1, weight)
+        weight = weight_of(sums_of(t - 1), t - 1, weight)
     with scope("bulk_wait"):
         bulk(t).wait_recv()
     with scope("residual"):
@@ -531,8 +558,7 @@
         gone.wait_recv()
         gone.wait_send()
     with scope("final"):
-        sums = sum_out[t] + jnp.sum(all_in[t], axis=0)
-        weight = weight_of(sums, t, None)
+        weight = weight_of(sums_of(t), t, None)
         stats_ref[0:1, :] = jnp.broadcast_to(weight, (1, 128))
         stats_ref[1:2, :] = jnp.maximum(sum_out[t], jnp.max(all_in[t], axis=0))
         stats_ref[2:8, :] = jnp.zeros((6, 128), F32)
@@ -591,11 +617,16 @@
             pltpu.VMEM((ITERS, 8, 128), F32),
             pltpu.VMEM((ITERS, 1, 128), F32),
             pltpu.VMEM((ITERS, len(OTHERS), 1, 128), F32),
+            pltpu.VMEM((ITERS, len(ORDER), 1, 128), F32),
+            pltpu.VMEM((ITERS, 1, 128), F32),
+            pltpu.VMEM((ITERS, len(ZV_ORDER), 1, 128), F32),
             dma((ITERS + 4,)),
             dma((ITERS,)),
             dma((ITERS,)),
             dma((ITERS, 3)),
             dma((ITERS, 3)),
+            dma((ITERS,)),
+            dma((ITERS,)),
             dma((ITERS,)),
             dma((ITERS,)),
             pltpu.SemaphoreType.REGULAR,

time: 76.4 us -> 75.1 us (0.983)
  Pallas kernels: 75.7 us -> 74.3 us
    pallas_call x1, Pallas kernels: 74 us -> 72.7 us  [shards(): pl.pallas_call(kernel, out_shape=(pltpu.VMEM(halves, F32), pltpu.VMEM((2,...]
where the time goes in v4:
time: 75.1 us; the launch traced here: 75 us
  Pallas kernels  74.3 us (99%)
    pallas_call x1, Pallas kernels, shards(): pl.pallas_call(kernel, out_shape=(pltpu.VMEM(halves, F32), pltpu.VMEM((2,...  72.7 us
    pallas_call x1, Pallas kernels, shards(): pl.pallas_call(finish, out_shape=(jax.ShapeDtypeStruct(flat_table, F32),...  1.63 us

profile of v4, /device:TPU:1, one launch (start us, length us, event | category | flops | bytes accessed | tf_op | source)
XLA Modules:
  0.0 75.0 jit_solution(2347906168959653128)
XLA Ops:
  0.6 72.7 %refine.1 = (f32[2,1088,128]{2,1,0:T(8,128)S(1)}, f32[2,1024,128]{2,1,0:T(8,128)S(1)}, f32[8,128]{1,0:T(8,128)S(1)}, f32[4,16]{1,0:T(4,128)S(1)}) custom-call(s32[4,16,128]{2,1,0:T(8,128)} %bitcast.5, f32[1024,256]{1,0:T(8,128)} %bitcast.4, f32[4,16,16,1024]{3,2,1,0:T(8,128)} %refined_hbm.1), custom_call_target="tpu_custom_call" | custom-call | tf_op jit(solution)/shard_map/refine/pallas_call | solution.py:591
  73.4 1.6 %finish.1 = (f32[1024,256]{1,0:T(8,128)}, f32[4,16]{1,0:T(4,128)}, f32[1,4]{1,0:T(1,128)}) custom-call(f32[2,1088,128]{2,1,0:T(8,128)S(1)} %get-tuple-element.10.tab, f32[2,1024,128]{2,1,0:T(8,128)S(1)} %get-tuple-element.11.flat, f32[8,128]{1,0:T(8,128)S(1)} %get-tuple-element.12.stats, f32[4,16]{1,0:T(4,128)S(1)} %get-tuple-element.13.errors), custom_call_target="tpu_custom_call" | custom-call | tf_op jit(solution)/shard_map/finish/pallas_call | solution.py:638

commit v5 on v4

--- a/solution.py
+++ b/solution.py
@@ -564,7 +564,8 @@
         stats_ref[2:8, :] = jnp.zeros((6, 128), F32)
 
 
-def finish(tab, flat, stats, errors, out_hbm, error_ref, worst_ref, out, out_sem):
+def finish(tab, flat, stats, errors, out_hbm, error_hbm, worst_hbm, out, worst, out_sem):
+    worst[...] = stats[1:2, 1 : ITERS + 1]
     stores = []
     for i in range(8):
         h, rows = i % 2, pl.ds(i // 2 * 256, 256)
@@ -574,8 +575,11 @@
         )
         store.start()
         stores.append(store)
-    error_ref[...] = errors[...]
-    worst_ref[...] = stats[1:2, 1 : ITERS + 1]
+        if i == 0:
+            stores.append(pltpu.make_async_copy(errors, error_hbm, out_sem.at[8]))
+            stores.append(pltpu.make_async_copy(worst, worst_hbm, out_sem.at[9]))
+            stores[1].start()
+            stores[2].start()
     for store in stores:
         store.wait()
 
@@ -643,8 +647,12 @@
             jax.ShapeDtypeStruct((1, ITERS), F32),
         ),
         in_specs=[vmem] * 4,
-        out_specs=(any_space, vmem, vmem),
-        scratch_shapes=[pltpu.VMEM((2, depth * width, 128), F32), dma((8,))],
+        out_specs=(any_space,) * 3,
+        scratch_shapes=[
+            pltpu.VMEM((2, depth * width, 128), F32),
+            pltpu.VMEM((1, ITERS), F32),
+            dma((10,)),
+        ],
         name="finish",
     )(*held)
     return table_out.reshape(table.shape), errors, worst.reshape(ITERS)

time: 75.1 us -> 74.5 us (level)
  no operation moved by 1% of the time
where the time goes in v5:
time: 74.5 us; the launch traced here: 74.4 us
  Pallas kernels  73.8 us (99%)
    pallas_call x1, Pallas kernels, shards(): pl.pallas_call(kernel, out_shape=(pltpu.VMEM(halves, F32), pltpu.VMEM((2,...  72.7 us

profile of v5, /device:TPU:1, one launch (start us, length us, event | category | flops | bytes accessed | tf_op | source)
XLA Modules:
  0.0 74.4 jit_solution(5542334997633947026)
XLA Ops:
  0.6 72.7 %refine.1 = (f32[2,1088,128]{2,1,0:T(8,128)S(1)}, f32[2,1024,128]{2,1,0:T(8,128)S(1)}, f32[8,128]{1,0:T(8,128)S(1)}, f32[4,16]{1,0:T(4,128)S(1)}) custom-call(s32[4,16,128]{2,1,0:T(8,128)} %bitcast.5, f32[1024,256]{1,0:T(8,128)} %bitcast.4, f32[4,16,16,1024]{3,2,1,0:T(8,128)} %refined_hbm.1), custom_call_target="tpu_custom_call" | custom-call | tf_op jit(solution)/shard_map/refine/pallas_call | solution.py:595
  73.4 1.1 %finish.1 = (f32[1024,256]{1,0:T(8,128)}, f32[4,16]{1,0:T(4,128)}, f32[1,4]{1,0:T(1,128)}) custom-call(f32[2,1088,128]{2,1,0:T(8,128)S(1)} %get-tuple-element.10.tab, f32[2,1024,128]{2,1,0:T(8,128)S(1)} %get-tuple-element.11.flat, f32[8,128]{1,0:T(8,128)S(1)} %get-tuple-element.12.stats, f32[4,16]{1,0:T(4,128)S(1)} %get-tuple-element.13.errors), custom_call_target="tpu_custom_call" | custom-call | tf_op jit(solution)/shard_map/finish/pallas_call | solution.py:642

commit v6 on v5

--- a/solution.py
+++ b/solution.py
@@ -112,6 +112,7 @@
     zm_in,
     zv_out,
     zv_in,
+    early,
     in_sem,
     bulk_send,
     bulk_recv,
@@ -526,7 +527,13 @@
             place_corner(res, t + 1)
             interpolate(res, mean_res, 8)
 
+    def largest_of(s):
+        largest = jnp.max(jnp.max(peak[s], axis=0), axis=0, keepdims=True)
+        return jnp.max(largest, axis=1, keepdims=True)
+
     t = ITERS - 1
+    with scope("maxima"):
+        early[...] = pack([jnp.zeros((1, 1), F32), *[largest_of(s) for s in range(t)]])
     with scope("sum_wait"):
         gone.wait_recv()
         weight = weight_of(sums_of(t - 1), t - 1, weight)
@@ -535,11 +542,9 @@
     with scope("residual"):
         squares = residuals(t, weight)
     with scope("sum_start"):
-        values = [jnp.sum(jnp.sum(squares, axis=0, keepdims=True), axis=1, keepdims=True)]
-        for s in range(ITERS):
-            largest = jnp.max(jnp.max(peak[s], axis=0), axis=0, keepdims=True)
-            values.append(jnp.max(largest, axis=1, keepdims=True))
-        sum_out[t] = pack(values)
+        total = jnp.sum(jnp.sum(squares, axis=0, keepdims=True), axis=1, keepdims=True)
+        row = jnp.where(lanes((1, 128)) == 0, total, early[...])
+        sum_out[t] = jnp.where(lanes((1, 128)) == ITERS, largest_of(t), row)
         gone = gather(t)
         pending.append(gone)
     with scope("relayout"):
@@ -624,6 +629,7 @@
             pltpu.VMEM((ITERS, len(ORDER), 1, 128), F32),
             pltpu.VMEM((ITERS, 1, 128), F32),
             pltpu.VMEM((ITERS, len(ZV_ORDER), 1, 128), F32),
+            pltpu.VMEM((1, 128), F32),
             dma((ITERS + 4,)),
             dma((ITERS,)),
             dma((ITERS,)),

time: 74.5 us -> 74.5 us (level)
  no operation moved by 1% of the time
where the time goes in v6:
time: 74.5 us; the launch traced here: 74.4 us
  Pallas kernels  73.8 us (99%)
    pallas_call x1, Pallas kernels, shards(): pl.pallas_call(kernel, out_shape=(pltpu.VMEM(halves, F32), pltpu.VMEM((2,...  72.7 us

profile of v6, /device:TPU:1, one launch (start us, length us, event | category | flops | bytes accessed | tf_op | source)
XLA Modules:
  0.0 74.4 jit_solution(3543086604531872625)
XLA Ops:
  0.6 72.7 %refine.1 = (f32[2,1088,128]{2,1,0:T(8,128)S(1)}, f32[2,1024,128]{2,1,0:T(8,128)S(1)}, f32[8,128]{1,0:T(8,128)S(1)}, f32[4,16]{1,0:T(4,128)S(1)}) custom-call(s32[4,16,128]{2,1,0:T(8,128)} %bitcast.5, f32[1024,256]{1,0:T(8,128)} %bitcast.4, f32[4,16,16,1024]{3,2,1,0:T(8,128)} %refined_hbm.1), custom_call_target="tpu_custom_call" | custom-call | tf_op jit(solution)/shard_map/refine/pallas_call | solution.py:600
  73.3 1.1 %finish.1 = (f32[1024,256]{1,0:T(8,128)}, f32[4,16]{1,0:T(4,128)}, f32[1,4]{1,0:T(1,128)}) custom-call(f32[2,1088,128]{2,1,0:T(8,128)S(1)} %get-tuple-element.10.tab, f32[2,1024,128]{2,1,0:T(8,128)S(1)} %get-tuple-element.11.flat, f32[8,128]{1,0:T(8,128)S(1)} %get-tuple-element.12.stats, f32[4,16]{1,0:T(4,128)S(1)} %get-tuple-element.13.errors), custom_call_target="tpu_custom_call" | custom-call | tf_op jit(solution)/shard_map/finish/pallas_call | solution.py:648
